TPU v7x, 256 devices: a whole 4x4x8 slice. The times are simulated.
256 devices in a mesh: rep: 1, dp: 256 (over x, y, z, core).
Axes of the slice: x: 4, y: 4, z: 8, core: 2. Of those that a mesh axis runs over, the one named last changes fastest.
Arguments:
- x: bfloat16 [256, 1024, 768], P(('rep', 'dp'))
- dy: bfloat16 [256, 1024, 768], P(('rep', 'dp'))
- w_gate: bfloat16 [2, 768, 6144], P(None, 'dp')
- w_up: bfloat16 [2, 768, 6144], P(None, 'dp')
- w_down: bfloat16 [2, 6144, 768], P(None, 'dp')
- m_w_gate: float32 [2, 768, 6144], P(None, 'dp')
- m_w_up: float32 [2, 768, 6144], P(None, 'dp')
- m_w_down: float32 [2, 6144, 768], P(None, 'dp')
- v_w_gate: float32 [2, 768, 6144], P(None, 'dp')
- v_w_up: float32 [2, 768, 6144], P(None, 'dp')
- v_w_down: float32 [2, 6144, 768], P(None, 'dp')
Outputs:
- output 1: bfloat16 [2, 768, 6144], P('rep', 'dp')
- output 2: bfloat16 [2, 768, 6144], P('rep', 'dp')
- output 3: bfloat16 [2, 6144, 768], P('rep', 'dp')
- output 4: float32 [2, 768, 6144], P('rep', 'dp')
- output 5: float32 [2, 768, 6144], P('rep', 'dp')
- output 6: float32 [2, 6144, 768], P('rep', 'dp')
- output 7: float32 [2, 768, 6144], P('rep', 'dp')
- output 8: float32 [2, 768, 6144], P('rep', 'dp')
- output 9: float32 [2, 6144, 768], P('rep', 'dp')
All inputs are finite; a program needn't handle non-finite values.
Results may differ from a plain program's by a relative error of at most 0.022.
Values are sent between devices in bfloat16 or wider.
A program may use at most 768 MiB of HBM per device.

v0:
```python
import jax
import jax.numpy as jnp
from jax import lax
from jax.sharding import PartitionSpec as P

NAMES = ("w_gate", "w_up", "w_down")


def matmul(a, w):
    return jnp.dot(a, w, preferred_element_type=jnp.float32).astype(jnp.bfloat16)


def normed(h):
    wide = h.astype(jnp.float32)
    scale = lax.rsqrt(jnp.mean(wide**2, -1, keepdims=True) + 1e-6)
    return (wide * scale).astype(jnp.bfloat16)


def layer(h, w):
    a = normed(h)
    gate = jnp.dot(a, w["w_gate"], preferred_element_type=jnp.float32)
    up = jnp.dot(a, w["w_up"], preferred_element_type=jnp.float32)
    return h + matmul((jax.nn.silu(gate) * up).astype(jnp.bfloat16), w["w_down"])


def adamw(w, m, v, g):
    m = 0.9 * m + 0.1 * g
    v = 0.95 * v + 0.05 * g * g
    step = m * lax.rsqrt(v + 1e-8) + 0.1 * w
    return (w - 0.02 * step).astype(jnp.bfloat16), m, v


def clipped(gradients, sum_of_squares, count):
    factor = jnp.minimum(1.0, 0.5 * lax.rsqrt(sum_of_squares / count + 1e-30))
    return [g * factor for g in gradients]


def solution(mesh):
    def fetched(weights, number):
        return {name: lax.all_gather(w[number], "dp", axis=0, tiled=True) for name, w in zip(NAMES, weights, strict=True)}

    def step(x, dy, *arrays):
        weights, m, v = (arrays[i : i + 3] for i in (0, 3, 6))
        layers = weights[0].shape[0]
        h, kept = x[0], []
        for number in range(layers):
            kept.append(h)
            h = layer(h, fetched(weights, number))
        by_h, mine = dy[0], [None] * layers
        for number in reversed(range(layers)):
            _, back = jax.vjp(lambda w, h: layer(h, w), fetched(weights, number), kept[number])
            by_w, by_h = back(by_h)
            mine[number] = [lax.psum_scatter(by_w[name], "dp", scatter_dimension=0, tiled=True) for name in NAMES]
        gradients = [jnp.stack([mine[number][i] for number in range(layers)]).astype(jnp.float32) for i in range(3)]
        squares = lax.psum(sum(jnp.sum(g * g) for g in gradients), "dp")
        gradients = clipped(gradients, squares, lax.psum(1, "dp") * sum(g.size for g in gradients))
        new = [adamw(w.astype(jnp.float32), m, v, g) for w, m, v, g in zip(weights, m, v, gradients, strict=True)]
        return tuple(one[which] for which in range(3) for one in new)

    states, cut = P(("rep", "dp"), None, None), P(None, "dp", None)
    return jax.shard_map(
        step,
        mesh=mesh,
        in_specs=(states, states) + (cut,) * 9,
        out_specs=(P("rep", "dp", None),) * 9,
        check_vma=False,
    )
```

profile of v0, /device:TPU:1, one launch (start us, length us, event | category | flops | bytes accessed | tf_op | source)
XLA Modules:
  0.0 2228.7 jit_solution(14178129168092634237)
XLA Ops:
  19.4 124.8 %all-gather.13.cloned.1.call-done = bf16[1,768,6144]{2,0,1:T(2,128)(2,1)} async-done(((bf16[1,3,6144]{2,0,1:T(2,128)(2,1)}), bf16[1,768,6144]{2,0,1:T(2,128)(2,1)}) %all-gather.13.cloned.1.call-update) | async-done | bytes 9437200 | tf_op jit(solution)/shard_map/all_gather | solution.py:40
  144.2 34.4 %fusion.31 = f32[1024,6144]{1,0:T(8,128)} fusion(bf16[1,768,6144]{2,0,1:T(2,128)(2,1)} %all-gather.13.cloned.1.call-done, bf16[1,1024,768]{1,2,0:T(8,128)(2,1)S(1)} %copy.54, f32[1024]{0:T(1024)S(1)} %add_rsqrt_fusion), kind=kOutput, calls=%fused_computation.42 | convolution fusion | flops 9666035712 | bytes 36179968 | tf_op jit(solution)/shard_map/dot_general | solution.py:21
  178.6 94.7 %all-gather.15.cloned.1.call-done = bf16[1,768,6144]{2,0,1:T(2,128)(2,1)} async-done(((bf16[1,3,6144]{2,0,1:T(2,128)(2,1)}), bf16[1,768,6144]{2,0,1:T(2,128)(2,1)}) %all-gather.15.cloned.1.call-update) | async-done | bytes 9437200 | tf_op jit(solution)/shard_map/all_gather | solution.py:40
  273.3 41.4 %multiply_convert_fusion.1 = (bf16[1024,6144]{1,0:T(8,128)(2,1)}, f32[1024,6144]{1,0:T(8,128)}) fusion(f32[1024,6144]{1,0:T(8,128)} %fusion.31, bf16[1,768,6144]{2,0,1:T(2,128)(2,1)} %all-gather.15.cloned.1.call-done, bf16[1,1024,768]{1,2,0:T(8,128)(2,1)S(1)} %copy.54, f32[1024]{0:T(1024)S(1)} %add_rsqrt_fusion), kind=kOutput, calls=%fused_computation.17 | convolution fusion | flops 9703784448 | bytes 73928704 | tf_op jit(solution)/shard_map/dot_general | solution.py:22
  314.7 78.4 %all-gather.17.cloned.1.call-done = bf16[1,6144,768]{2,1,0:T(8,128)(2,1)} async-done(((bf16[1,24,768]{2,1,0:T(8,128)(2,1)}), bf16[1,6144,768]{2,1,0:T(8,128)(2,1)}) %all-gather.17.cloned.1.call-update) | async-done | bytes 9437200 | tf_op jit(solution)/shard_map/all_gather | solution.py:40
  393.1 16.0 fusion.47
  409.1 103.3 %all-gather.21.cloned.1.call-done = bf16[1,6144,768]{2,1,0:T(8,128)(2,1)} async-done(((bf16[1,24,768]{2,1,0:T(8,128)(2,1)}), bf16[1,6144,768]{2,1,0:T(8,128)(2,1)}) %all-gather.21.cloned.1.call-update) | async-done | bytes 9437200 | tf_op jit(solution)/shard_map/all_gather | solution.py:40
  528.0 113.0 %all-gather.23.cloned.1.call-done = bf16[1,768,6144]{2,0,1:T(2,128)(2,1)} async-done(((bf16[1,3,6144]{2,0,1:T(2,128)(2,1)}), bf16[1,768,6144]{2,0,1:T(2,128)(2,1)}) %all-gather.23.cloned.1.call-update) | async-done | bytes 9437200 | tf_op jit(solution)/shard_map/all_gather | solution.py:40
  641.0 34.8 %fusion.21 = f32[1024,6144]{1,0:T(8,128)} fusion(bf16[1,768,6144]{2,0,1:T(2,128)(2,1)} %all-gather.23.cloned.1.call-done, bf16[1024,768]{0,1:T(8,128)(2,1)S(1)} %get-tuple-element.58, f32[1024]{0:T(1024)S(1)} %fusion.96), kind=kOutput, calls=%fused_computation.32 | convolution fusion | flops 9666035712 | bytes 36179968 | tf_op jit(solution)/shard_map/jvp()/dot_general | solution.py:22
  675.8 94.2 %all-gather.19.cloned.1.call-done = bf16[1,768,6144]{2,0,1:T(2,128)(2,1)} async-done(((bf16[1,3,6144]{2,0,1:T(2,128)(2,1)}), bf16[1,768,6144]{2,0,1:T(2,128)(2,1)}) %all-gather.19.cloned.1.call-update) | async-done | bytes 9437200 | tf_op jit(solution)/shard_map/all_gather | solution.py:40
  770.0 41.9 %fusion.2 = (bf16[1024,6144]{1,0:T(8,128)(2,1)}, f32[1024,6144]{1,0:T(8,128)}) fusion(f32[1024,6144]{1,0:T(8,128)} %fusion.21, bf16[1024,6144]{1,0:T(8,128)(2,1)} %convolution_convert_fusion.1, bf16[1,768,6144]{2,0,1:T(2,128)(2,1)} %all-gather.19.cloned.1.call-done, bf16[1024,768]{0,1:T(8,128)(2,1)S(1)} %get-tuple-element.58, f32[1024]{0:T(1024)S(1)} %fusion.96), kind=kOutput, calls=%fused_computation.8 | convolution fusion | flops 9741533184 | bytes 86511616 | tf_op jit(solution)/shard_map/jvp()/dot_general | solution.py:21
  811.9 23.6 %fusion.50 = bf16[1024,768]{0,1:T(8,128)(2,1)} fusion(bf16[1024,6144]{1,0:T(8,128)(2,1)} %get-tuple-element.59, bf16[1,768,6144]{2,0,1:T(2,128)(2,1)} %all-gather.19.cloned.1.call-done), kind=kOutput, calls=%fused_computation.67 | convolution fusion | flops 9663676416 | bytes 23592960 | tf_op jit(solution)/shard_map/transpose(jvp())/dot_general | solution.py:21
  835.5 35.9 %fusion.49 = (f32[1024]{0:T(1024)S(1)}, bf16[1024,768]{0,1:T(8,128)(2,1)}) fusion(bf16[1024,768]{0,1:T(8,128)(2,1)S(1)} %get-tuple-element.58, bf16[1024,768]{0,1:T(8,128)(2,1)} %fusion.50, bf16[1,768,6144]{2,0,1:T(2,128)(2,1)} %all-gather.23.cloned.1.call-done, bf16[1024,6144]{1,0:T(8,128)(2,1)} %convolution_convert_fusion.1, ...), kind=kOutput, calls=%fused_computation.66 | convolution fusion | flops 9706142720 | bytes 51908608 | tf_op jit(solution)/shard_map/transpose(jvp())/dot_general | solution.py:22
  875.1 17.6 convolution_convert_fusion.2
  892.7 20.9 fusion.19
  913.7 24.7 %fusion.18 = bf16[6144,768]{1,0:T(8,128)(2,1)} fusion(f32[1024,6144]{1,0:T(8,128)} %fusion.21, bf16[1,1024,768]{2,1,0:T(8,128)(2,1)S(1)} %copy-done.3, f32[1024,6144]{1,0:T(8,128)} %get-tuple-element.60), kind=kOutput, calls=%fused_computation.27 | convolution fusion | flops 9706143744 | bytes 61341696 | tf_op jit(solution)/shard_map/transpose(jvp())/dot_general | solution.py:10
  938.4 16.8 convolution_convert_fusion.3
  955.3 16.2 convolution_convert_fusion
  971.5 20.6 fusion.20
  992.1 27.6 %fusion.15 = bf16[768,6144]{1,0:T(8,128)(2,1)} fusion(f32[1024,6144]{1,0:T(8,128)} %fusion.31, f32[1024,6144]{1,0:T(8,128)} %get-tuple-element.56, bf16[1024,6144]{1,0:T(8,128)(2,1)} %convolution_convert_fusion, bf16[1,1024,768]{1,2,0:T(8,128)(2,1)S(1)} %copy-done.1, f32[1024]{0:T(1024)S(1)} %copy-done.9), kind=kOutput, calls=%fused_computation.26 | convolution fusion | flops 9739960320 | bytes 73928704 | tf_op jit(solution)/shard_map/transpose(jvp())/dot_general | solution.py:21
  1019.8 268.9 %reduce-scatter.3.cloned.1.call-done = bf16[24,768]{1,0:T(8,128)(2,1)} async-done(((bf16[6144,768]{1,0:T(8,128)(2,1)}), bf16[24,768]{1,0:T(8,128)(2,1)}) %reduce-scatter.3.cloned.1.call-update) | async-done | bytes 36880 | tf_op jit(solution)/shard_map/reduce_scatter | solution.py:53
  1288.8 408.5 %reduce-scatter.5.cloned.1.call-done = bf16[24,768]{1,0:T(8,128)(2,1)} async-done(((bf16[6144,768]{1,0:T(8,128)(2,1)}), bf16[24,768]{1,0:T(8,128)(2,1)}) %reduce-scatter.5.cloned.1.call-update) | async-done | bytes 36880 | tf_op jit(solution)/shard_map/reduce_scatter | solution.py:53
  1698.7 433.1 %all-reduce.7.cloned.1.call-done = (bf16[768,6144]{1,0:T(8,128)(2,1)}, bf16[768,6144]{1,0:T(8,128)(2,1)}, bf16[768,6144]{1,0:T(8,128)(2,1)}, bf16[768,6144]{1,0:T(8,128)(2,1)}) async-done(((bf16[768,6144]{1,0:T(8,128)(2,1)}, bf16[768,6144]{1,0:T(8,128)(2,1)}, bf16[768,6144]{1,0:T(8,128)(2,1)}, bf16[768,6144]{1,0:T(8,128)(2,1)}), (bf16[768,6144]{1,0:T(8,128)(2,1)}, bf16[768,6144]{1,0:T(8,128)(2,1)}, ...) | async-done | bytes 37748752
  2137.4 76.9 %psum.7 = f32[]{:T(128)} all-reduce(f32[]{:T(128)S(6)} %add.99), channel_id=1, replica_groups=mesh['rep'=1,'dp'=256] {'dp'}, use_global_device_ids=true, to_apply=%region_12.13 | all-reduce | flops 1 | bytes 8 | tf_op jit(solution)/shard_map/psum | solution.py:55
  (77 shorter events, 43.6 us)
Async XLA Ops:
  7.2 137.0 %all-gather.13.cloned.1.call-start = ((), (), s32[]{:S(2)}) async-start(), calls=%async_computation.4 | async-start | bytes 18948096 | tf_op jit(solution)/shard_map/all_gather | solution.py:40
  9.0 264.3 %all-gather.15.cloned.1.call-start = ((), (), s32[]{:S(2)}) async-start(), calls=%async_computation.5 | async-start | bytes 18948096 | tf_op jit(solution)/shard_map/all_gather | solution.py:40
  10.8 382.3 %all-gather.17.cloned.1.call-start = ((), (), s32[]{:S(2)}) async-start(), calls=%async_computation.6 | async-start | bytes 9474048 | tf_op jit(solution)/shard_map/all_gather | solution.py:40
  12.3 500.1 %all-gather.21.cloned.1.call-start = ((), (), s32[]{:S(2)}) async-start(), calls=%async_computation.8 | async-start | bytes 9474048 | tf_op jit(solution)/shard_map/all_gather | solution.py:40
  12.9 628.2 %all-gather.23.cloned.1.call-start = ((), (), s32[]{:S(2)}) async-start(), calls=%async_computation.9 | async-start | bytes 18948096 | tf_op jit(solution)/shard_map/all_gather | solution.py:40
  13.5 756.5 %all-gather.19.cloned.1.call-start = ((), (), s32[]{:S(2)}) async-start(), calls=%async_computation.7 | async-start | bytes 18948096 | tf_op jit(solution)/shard_map/all_gather | solution.py:40
  14.1 1274.7 %reduce-scatter.3.cloned.1.call-start = ((), (), s32[]{:S(2)}) async-start(), calls=%async_computation.2 | async-start | bytes 9474048 | tf_op jit(solution)/shard_map/reduce_scatter | solution.py:53
  15.8 377.3 %copy-start = (bf16[1,1024,768]{1,2,0:T(8,128)(2,1)}, bf16[1,1024,768]{1,2,0:T(8,128)(2,1)S(1)}, u32[]{:S(2)}) copy-start(bf16[1,1024,768]{1,2,0:T(8,128)(2,1)S(1)} %copy.54) | copy-start | bytes 4718596
  19.4 253.9 %copy-start.8 = (f32[1024]{0:T(1024)}, f32[1024]{0:T(1024)S(1)}, u32[]{:S(2)}) copy-start(f32[1024]{0:T(1024)S(1)} %add_rsqrt_fusion) | copy-start | bytes 12292
  835.5 35.9 %copy-start.2 = (bf16[1,1024,768]{1,2,0:T(8,128)(2,1)S(1)}, bf16[1,1024,768]{1,2,0:T(8,128)(2,1)}, u32[]{:S(2)}) copy-start(bf16[1,1024,768]{1,2,0:T(8,128)(2,1)} %copy.55) | copy-start | bytes 4718596
  892.7 21.0 copy-start.3
  892.7 804.6 %reduce-scatter.5.cloned.1.call-start = ((), (), s32[]{:S(2)}) async-start(), calls=%async_computation.3 | async-start | bytes 9474048 | tf_op jit(solution)/shard_map/reduce_scatter | solution.py:53
  938.4 16.9 copy-start.5
  938.4 1193.4 %all-reduce.7.cloned.1.call-start = ((), (), s32[]{:S(2)}) async-start(), calls=%async_computation.10 | async-start | bytes 75497472
  955.3 16.2 copy-start.9
  1019.7 1195.2 %copy-start.6 = (bf16[2,3,6144]{2,0,1:T(2,128)(2,1)S(1)}, bf16[2,3,6144]{2,0,1:T(2,128)(2,1)}, u32[]{:S(2)}) copy-start(bf16[2,3,6144]{2,0,1:T(2,128)(2,1)} %param.14) | copy-start | bytes 221188
  1019.7 1195.3 %copy-start.11 = (f32[2,3,6144]{2,0,1:T(2,128)S(1)}, f32[2,3,6144]{2,0,1:T(2,128)}, u32[]{:S(2)}) copy-start(f32[2,3,6144]{2,0,1:T(2,128)} %param.20) | copy-start | bytes 442372
  1019.7 1195.3 %copy-start.12 = (f32[2,3,6144]{2,0,1:T(2,128)S(1)}, f32[2,3,6144]{2,0,1:T(2,128)}, u32[]{:S(2)}) copy-start(f32[2,3,6144]{2,0,1:T(2,128)} %param.17) | copy-start | bytes 442372
  1019.7 1198.0 %copy-start.7 = (bf16[2,3,6144]{2,0,1:T(2,128)(2,1)S(1)}, bf16[2,3,6144]{2,0,1:T(2,128)(2,1)}, u32[]{:S(2)}) copy-start(bf16[2,3,6144]{2,0,1:T(2,128)(2,1)} %param.13) | copy-start | bytes 221188
  1019.7 1198.0 %copy-start.13 = (f32[2,3,6144]{2,0,1:T(2,128)S(1)}, f32[2,3,6144]{2,0,1:T(2,128)}, u32[]{:S(2)}) copy-start(f32[2,3,6144]{2,0,1:T(2,128)} %param.19) | copy-start | bytes 442372
  1019.8 1198.0 %copy-start.14 = (f32[2,3,6144]{2,0,1:T(2,128)S(1)}, f32[2,3,6144]{2,0,1:T(2,128)}, u32[]{:S(2)}) copy-start(f32[2,3,6144]{2,0,1:T(2,128)} %param.16) | copy-start | bytes 442372
  1019.8 1200.6 %copy-start.10 = (bf16[2,24,768]{2,1,0:T(8,128)(2,1)S(1)}, bf16[2,24,768]{2,1,0:T(8,128)(2,1)}, u32[]{:S(2)}) copy-start(bf16[2,24,768]{2,1,0:T(8,128)(2,1)} %param.15) | copy-start | bytes 221188
  1019.8 1200.6 %copy-start.15 = (f32[2,24,768]{2,1,0:T(8,128)S(1)}, f32[2,24,768]{2,1,0:T(8,128)}, u32[]{:S(2)}) copy-start(f32[2,24,768]{2,1,0:T(8,128)} %param.21) | copy-start | bytes 442372
  1019.8 1200.6 %copy-start.16 = (f32[2,24,768]{2,1,0:T(8,128)S(1)}, f32[2,24,768]{2,1,0:T(8,128)}, u32[]{:S(2)}) copy-start(f32[2,24,768]{2,1,0:T(8,128)} %param.18) | copy-start | bytes 442372
  (2 other events, 17.4 us)
Sparse Core Ops, SparseCore 0:
  12.4 131.7 all-gather.12
  148.6 124.6 all-gather.14
  277.8 115.2 all-gather.16
  397.4 114.9 all-gather.20
  516.7 124.3 all-gather.22
  645.3 124.6 all-gather.18
  892.8 395.9 reduce-scatter.2
  1294.9 402.3 reduce-scatter.4
  1703.7 428.0 all-reduce.6
where the time goes:
time: 2240 us; the launch traced here: 2230 us
  waiting for transfers between devices  1720 us (77%)
  matrix products  388 us (17%)
  blocking collectives  76.9 us (3%)
    reduce_scatter x2, waiting for transfers between devices, step(): lax.psum_scatter(by_w[name], 'dp', scatter_dimension=0, tiled=True)  677 us
    all_gather x6, waiting for transfers between devices, fetched(): lax.all_gather(w[number], 'dp', axis=0, tiled=True)  608 us
    unnamed x10, waiting for transfers between devices  435 us
    dot_general x5, matrix products, layer(): up = jnp.dot(a, w['w_up'], preferred_element_type=jnp.float32)  154 us
    dot_general x5, matrix products, layer(): gate = jnp.dot(a, w['w_gate'], preferred_element_type=jnp.float32)  144 us
    dot_general x5, matrix products, matmul(): jnp.dot(a, w, preferred_element_type=jnp.float32).astype(jnp.bfloat16)  90.1 us
    psum x1, blocking collectives, step(): squares = lax.psum(sum((jnp.sum(g * g) for g in gradients)), 'dp')  76.9 us
  transfers between devices with their start and end apart: 9, of which 9 were waited for; matrix products, arithmetic and copies ran while one was open for 13% of the time, Pallas kernels for 0%

commit v1 on v0

v1 whole, which is shorter than its diff:
```python
import functools
import itertools
import jax
import jax.numpy as jnp
from jax import lax
from jax.experimental import pallas as pl
from jax.experimental.pallas import tpu as pltpu
from jax.sharding import PartitionSpec as P

DIMS = (4, 4, 8, 2)
T = 3
CH, CL = 24, 256
ORDERS = ((0, 1, 2), (1, 2, 0), (2, 0, 1))
f32, bf16 = jnp.float32, jnp.bfloat16
ALL = slice(None)
LANES = CL // 2


def coords():
    me = lax.axis_index("dp")
    c = lax.rem(me, DIMS[3])
    r = lax.div(me, DIMS[3])
    z = lax.rem(r, DIMS[2])
    r = lax.div(r, DIMS[2])
    y = lax.rem(r, DIMS[1])
    x = lax.div(r, DIMS[1])
    return [x, y, z, c]


def flat(co):
    return ((co[0] * DIMS[1] + co[1]) * DIMS[2] + co[2]) * DIMS[3] + co[3]


def moved(co, axis, by):
    n = DIMS[axis]
    out = list(co)
    out[axis] = lax.rem(co[axis] + (by + n), n)
    return out


def group_peers(co):
    zs = min(4, DIMS[2])
    base = lax.div(co[2], zs) * zs
    mine = lax.rem(co[2], zs) * DIMS[3] + co[3]
    return zs * DIMS[3], base, mine


def member(co, base, j):
    out = list(co)
    out[2] = base + lax.div(j, DIMS[3])
    out[3] = lax.rem(j, DIMS[3])
    return out


def greet(co, extra=()):
    barrier = pltpu.get_barrier_semaphore()
    peers = [moved(co, a, d) for a in range(3) for d in (1, -1)]
    peers += [co[:3] + [(co[3] + k) % DIMS[3]] for k in range(1, DIMS[3])]
    peers += list(extra)
    for peer in peers:
        pl.semaphore_signal(barrier, inc=1, device_id={"dp": flat(peer)})
    pl.semaphore_wait(barrier, len(peers))


def side(by):
    return (1 - by) // 2


def columns(half):
    return ALL if half is ALL else pl.ds(half * LANES, LANES)


def remote(src, dst, ssem, rsem, co):
    return pltpu.make_async_remote_copy(src_ref=src, dst_ref=dst, send_sem=ssem, recv_sem=rsem, device_id={"dp": flat(co)})


def at(ref, sel, core, cols=ALL):
    index = [ALL] + list(sel)
    if core is not ALL:
        index.append(core)
    if cols is not ALL:
        index += [ALL, cols]
    return ref.at[tuple(index)]


HOP = 3.0
RATE = 46.6e3
CHUNK_BYTES = T * CH * CL * 2


def gather_ticks(stream, ref, own, order, co, ssem, rsem, dsend, drecv, local, start=0.0):
    partner = co[:3] + [1 - co[3]]
    ticks, sends, d2d = [], [], []
    time = start
    n_copy = itertools.count()
    n_d2d = itertools.count()

    def forward(block):
        copy = remote(block, block, dsend.at[next(n_d2d)], drecv.at[0], partner)
        copy.start()
        d2d.append(copy)

    mine = at(ref, co[:3], co[3])
    keep = pltpu.make_async_copy(own, mine, local.at[0])
    arrived = []
    for k, axis in enumerate(order):
        n = DIMS[axis]
        done, last = order[:k], k == len(order) - 1
        blocks = 1
        for a in done:
            blocks *= DIMS[a]

        def block(pos, half=ALL, done=done, axis=axis):
            sel = [ALL if a in done else co[a] for a in range(3)]
            sel[axis] = pos
            cols = ALL
            if half is not ALL:
                if done:
                    h = DIMS[done[0]] // 2
                    sel[done[0]] = pl.ds(half * h, h)
                else:
                    cols = columns(half)
            return at(ref, sel, co[3], cols)

        for s in range(1, n // 2 + 1):
            final = s == n // 2

            def tick(k=k, s=s, axis=axis, final=final, last=last, block=block):
                came = list(arrived)
                arrived.clear()
                if k == 0 and s == 1:
                    keep.start()
                if k == 1 and s == 1:
                    keep.wait()
                for copy, got in came:
                    copy.wait_recv()
                for by in (1, -1):
                    pos = moved(co, axis, -by * (s - 1))[axis]
                    half = side(by) if final else ALL
                    target = block(pos, half)
                    source = target
                    if k == 0 and s == 1:
                        source = own.at[:, :, columns(half)]
                    i = next(n_copy)
                    copy = remote(source, target, ssem.at[i], rsem.at[i], moved(co, axis, by))
                    copy.start()
                    sends.append(copy)
                    got = block(moved(co, axis, -by * s)[axis], half)
                    arrived.append((copy, got))
                if last:
                    if s == 1:
                        forward(block(co[axis]))
                    else:
                        for copy, got in came:
                            forward(got)

            ticks.append((time, tick))
            time += HOP + blocks * CHUNK_BYTES * (0.5 if final else 1.0) / RATE

    def finish():
        for copy, got in arrived:
            copy.wait_recv()
            forward(got)

    def drain():
        half = at(ref, [ALL] * 3, 1 - co[3])
        pltpu.make_async_copy(half, half, drecv.at[0]).wait()
        for copy in sends + d2d:
            copy.wait_send()

    ticks.append((time, finish))
    ticks.append((time + 5.0, drain))
    return ticks


def run(ticks):
    for _, tick in sorted(ticks, key=lambda t: t[0]):
        tick()


def scatter_scratch(order):
    n2, n3 = DIMS[order[1]], DIMS[order[2]]
    whole = (T,) + DIMS[:3] + (CH, CL)
    return [
        pltpu.VMEM(whole, bf16),
        pltpu.VMEM(whole, bf16),
        pltpu.VMEM(whole, bf16),
        pltpu.VMEM((T, n2, n3, CH, CL), f32),
        pltpu.VMEM((T, n2, n3, CH, CL), bf16),
        pltpu.VMEM((T, n2, n3, CH, CL), bf16),
        pltpu.VMEM((T, n3, CH, CL), bf16),
        pltpu.SemaphoreType.DMA((3, DIMS[order[0]])),
        pltpu.SemaphoreType.DMA((2, 16)),
    ]


SCATTER_SCRATCH = 9


def scatter_ticks(partial, order, co, scratch, out, start=0.0):
    kept, other, came1, total, going, came2, came3, load, ring = scratch
    b1, b2, b3 = order
    n1, n2, n3 = (DIMS[a] for a in order)
    p1, p2, p3 = (co[a] for a in order)
    partner = co[:3] + [1 - co[3]]
    ticks, sends = [], []
    n_copy = itertools.count()
    time = start

    def sel(q, i=ALL, j=ALL):
        s = [ALL] * 3
        s[b1], s[b2], s[b3] = q, i, j
        return s

    def place(ref, s):
        return ref.at[tuple([ALL] + s)]

    offsets = [n1 // 2] + [d * k for k in range(n1 // 2 - 1, 0, -1) for d in (1, -1)] + [0]
    loads = {}

    def begin():
        for i, off in enumerate(offsets):
            q = moved(co, b1, off)[b1]
            here = pltpu.make_async_copy(at(partial, sel(q), co[3]), place(kept, sel(q)), load.at[0, i])
            there = remote(at(partial, sel(q), 1 - co[3]), place(other, sel(q)), load.at[1, i], load.at[2, i], partner)
            there.start()
            here.start()
            loads[off] = [here, there]
            sends.append(there)

    def ready(off):
        off = -off if off == -(n1 // 2) else off
        if off in loads:
            here, there = loads.pop(off)
            here.wait()
            there.wait_recv()

    def add(count, spots, dst, srcs):
        def body(m, _):
            spot = spots(m)
            for t in range(T):
                ref, index = dst(t, *spot)
                value = sum(r[i].astype(f32) for r, i in (s(t, *spot) for s in srcs))
                ref[index] = value.astype(ref.dtype)
            return 0

        lax.fori_loop(0, count, body, 0)

    def phase1(ref, q):
        def spot(t, i, j):
            s = sel(q, i, j)
            return ref, (t, s[0], s[1], s[2])

        return spot

    def phase2(ref, q):
        return lambda t, j: (ref, (t, q, j))

    def phase3(ref, q, first=()):
        return lambda t: (ref, (t,) + tuple(first) + (q,))

    def step(axis, n, p, s, sum_into, view, slots):
        out = []
        for by in (1, -1):
            off = by * (n // 2 + 1 - s)
            q = moved(co, axis, off)[axis]
            half = side(by) if s == 1 else ALL
            mine = side(by)
            sum_into(q, half, s, mine, off)
            if by == -1 and s == n // 2:
                slot = moved(co, axis, by + n // 2)[axis]
            else:
                slot = q
            i = next(n_copy)
            copy = remote(view(q, half), slots(slot, half), ring.at[0, i], ring.at[1, i], moved(co, axis, by))
            copy.start()
            sends.append(copy)
            out.append(copy)
        return out

    arrived = []

    def await_arrived():
        for copy in arrived:
            copy.wait_recv()
        arrived.clear()

    def halves(n, half):
        return (0, n) if half is ALL else (half * (n // 2), n // 2)

    def sum1(q, half, s, mine, off):
        ready(off)

        def part(lo, size, with_sum):
            def spots(m):
                return lo + lax.div(m, n3), lax.rem(m, n3)

            srcs = [phase1(kept, q), phase1(other, q)] + ([phase1(came1, q)] if with_sum else [])
            add(size * n3, spots, phase1(kept, q), srcs)

        if s == 1:
            part(*halves(n2, half), False)
        elif s == 2:
            part(*halves(n2, mine), True)
            part(*halves(n2, 1 - mine), False)
        else:
            part(0, n2, True)

    def cut1(ref):
        def view(q, half):
            lo, size = halves(n2, half)
            return place(ref, sel(q, ALL if half is ALL else pl.ds(lo, size)))

        return view

    def end1():
        await_arrived()
        ready(0)
        mine, far = p1, moved(co, b1, n1 // 2)[b1]
        add(n2 * n3, lambda m: (lax.div(m, n3), lax.rem(m, n3)), lambda t, i, j: (total, (t, i, j)),
            [phase1(kept, mine), phase1(other, mine), phase1(came1, mine), phase1(came1, far)])

    def sum2(q, half, s, mine, off):
        def part(lo, size, with_sum):
            srcs = [phase2(total, q)] + ([phase2(came2, q)] if with_sum else [])
            add(size, lambda m: (lo + m,), phase2(going, q), srcs)

        if s == 1:
            part(*halves(n3, half), False)
        elif s == 2:
            part(*halves(n3, mine), True)
            part(*halves(n3, 1 - mine), False)
        else:
            part(0, n3, True)

    def cut2(ref):
        def view(q, half):
            lo, size = halves(n3, half)
            return ref.at[:, q, pl.ds(lo, size)]

        return view

    def end2():
        await_arrived()
        far = moved(co, b2, n2 // 2)[b2]
        add(n3, lambda m: (m,), phase2(total, p2), [phase2(total, p2), phase2(came2, p2), phase2(came2, far)])

    def sum3(q, half, s, mine, off):
        def part(cols, with_sum):
            for t in range(T):
                value = total[t, p2, q, :, cols]
                if with_sum:
                    value = value + came3[t, q, :, cols].astype(f32)
                going[t, p2, q, :, cols] = value.astype(bf16)

        if s == 1:
            part(columns(half), False)
        elif s == 2:
            part(columns(mine), True)
            part(columns(1 - mine), False)
        else:
            part(ALL, True)

    def end3():
        await_arrived()
        far = moved(co, b3, n3 // 2)[b3]
        for t in range(T):
            value = total[t, p2, p3] + came3[t, p3].astype(f32) + came3[t, far].astype(f32)
            out[t] = value.astype(bf16).astype(f32)

    def cut3(ref, first):
        def view(q, half):
            cols = columns(half)
            index = (ALL,) + tuple(first) + (q, ALL, cols)
            return ref.at[index]

        return view

    ticks.append((time, begin))
    time += 2.0
    phases = (
        (b1, n1, p1, sum1, cut1(kept), cut1(came1), end1, n2 * n3),
        (b2, n2, p2, sum2, cut2(going), cut2(came2), end2, n3),
        (b3, n3, p3, sum3, cut3(going, (p2,)), cut3(came3, ()), end3, 1),
    )
    for axis, n, p, sum_into, view, slots, end, blocks in phases:
        for s in range(1, n // 2 + 1):

            def tick(axis=axis, n=n, p=p, s=s, sum_into=sum_into, view=view, slots=slots):
                await_arrived()
                arrived.extend(step(axis, n, p, s, sum_into, view, slots))

            ticks.append((time, tick))
            time += HOP + 0.5 + blocks * CHUNK_BYTES * (0.5 if s == 1 else 1.0) / RATE
        ticks.append((time, end))
        time += 0.2

    def drain():
        for copy in sends:
            copy.wait_send()

    ticks.append((time + 1.0, drain))
    return ticks


def plane_sum(co, axes, mine, slots, send, recv):
    n = 1
    for a in axes:
        n *= DIMS[a]
    me = 0
    for a in axes:
        me = me * DIMS[a] + co[a]
    slots[me] = mine
    copies = []
    for k in range(1, n):
        copy = remote(slots.at[me], slots.at[me], send.at[k], recv.at[0], plane_peer(co, axes, me, k, n))
        copy.start()
        copies.append(copy)
    rest = slots.at[pl.ds(0, n - 1)]
    pltpu.make_async_copy(rest, rest, recv.at[0]).wait()
    for copy in copies:
        copy.wait_send()
    return jnp.sum(slots[...], axis=0)


def plane_peer(co, axes, me, k, n):
    other = lax.rem(me + k, n)
    peer = list(co)
    for a in reversed(axes):
        peer[a] = lax.rem(other, DIMS[a])
        other = lax.div(other, DIMS[a])
    return peer


def plane_peers(co, axes):
    n, me = 1, 0
    for a in axes:
        n *= DIMS[a]
        me = me * DIMS[a] + co[a]
    return [plane_peer(co, axes, me, k, n) for k in range(1, n)]


SUM_PLANES = ((2, 3), (0, 1))


def gather_kernel(layers, rows_ref, down_ref, *rest):
    outs = rest[: 3 * layers]
    got, wide, chunk, xsend, xrecv, sems, local = rest[3 * layers :]
    co = coords()
    size, base, mine = group_peers(co)
    peers = [member(co, base, lax.rem(mine + k, size)) for k in range(1, size)]
    greet(co, peers)
    copies = []
    for k in range(1, size):
        j = lax.rem(mine + k, size)
        copy = remote(rows_ref.at[j], got.at[mine], xsend.at[k], xrecv.at[0], member(co, base, j))
        copy.start()
        copies.append(copy)
    got[pl.ds(mine, 1)] = rows_ref[pl.ds(mine, 1)]
    for l in range(layers):
        chunk[3 * l + 2] = down_ref[l]
    rest_of = got.at[pl.ds(0, size - 1)]
    pltpu.make_async_copy(rest_of, rest_of, xrecv.at[0]).wait()
    per = CH // size
    for l in range(layers):
        for i in range(2):
            row = (2 * l + i) * per
            for t in range(T):
                for j in range(size):
                    wide[t, pl.ds(per * j, per), :] = got[j, t, pl.ds(row, per), :]
            chunk[3 * l + i] = wide[...].astype(bf16)
    for copy in copies:
        copy.wait_send()
    ticks = []
    for l in range(layers):
        for i in range(3):
            n = 3 * l + i
            ticks += gather_ticks(n, outs[n], chunk.at[n], ORDERS[i], co, sems.at[n, 0], sems.at[n, 1], sems.at[n, 2], local.at[n, pl.ds(0, 1)],
                                  local.at[n, pl.ds(1, 1)], start=2.0 * l)
    run(ticks)


def gather(layers, rows, down):
    size = rows.shape[0]
    whole = jax.ShapeDtypeStruct((T,) + DIMS + (CH, CL), bf16)
    return pl.pallas_call(
        functools.partial(gather_kernel, layers),
        out_shape=[whole] * (3 * layers),
        in_specs=[pl.BlockSpec(memory_space=pltpu.VMEM)] * 2,
        out_specs=[pl.BlockSpec(memory_space=pltpu.HBM)] * (3 * layers),
        scratch_shapes=[
            pltpu.VMEM(rows.shape, f32),
            pltpu.VMEM((T, CH, CL), f32),
            pltpu.VMEM((3 * layers, T, CH, CL), bf16),
            pltpu.SemaphoreType.DMA((size,)),
            pltpu.SemaphoreType.DMA((1,)),
            pltpu.SemaphoreType.DMA((3 * layers, 3, 16)),
            pltpu.SemaphoreType.DMA((3 * layers, 2)),
        ],
        compiler_params=pltpu.CompilerParams(collective_id=1, has_side_effects=True, vmem_limit_bytes=30 * 2**20),
        name="gather",
    )(rows, down)


def scatter_kernel(with_total, *refs):
    partials, refs = refs[:3], refs[3:]
    if with_total:
        before, refs = refs[0], refs[1:]
    rows_out, down_out, squares_out, refs = refs[0], refs[1], refs[2], refs[3:]
    scratch, refs = refs[: 3 * SCATTER_SCRATCH], refs[3 * SCATTER_SCRATCH :]
    sums, going, xsend, xrecv = refs[:4]
    co = coords()
    size, base, mine = group_peers(co)
    peers = [member(co, base, lax.rem(mine + k, size)) for k in range(1, size)]
    extra = [p for axes in SUM_PLANES for p in plane_peers(co, axes)] if with_total else []
    greet(co, peers + extra)
    ticks = []
    for i in range(3):
        mine_scratch = scratch[SCATTER_SCRATCH * i : SCATTER_SCRATCH * (i + 1)]
        ticks += scatter_ticks(partials[i], ORDERS[i][::-1], co, mine_scratch, sums.at[i])
    run(ticks)
    down_out[...] = sums[2]
    per = CH // size
    for i in range(2):
        for t in range(T):
            for j in range(size):
                going[j, t, pl.ds(per * i, per), :] = sums[i, t, pl.ds(per * j, per), :]
    copies = []
    for k in range(1, size):
        j = lax.rem(mine + k, size)
        copy = remote(going.at[j], rows_out.at[mine], xsend.at[k], xrecv.at[0], member(co, base, j))
        copy.start()
        copies.append(copy)
    rows_out[pl.ds(mine, 1)] = going[pl.ds(mine, 1)]
    square = sums[...] * sums[...]
    square = jnp.sum(square.reshape(3 * T * CH // 8, 8, CL), axis=0)
    square = square[:, : CL // 2] + square[:, CL // 2 :]
    if with_total:
        square = square + before[...]
        slots_a, slots_b, vsend, vrecv = refs[4:]
        square = plane_sum(co, SUM_PLANES[0], square, slots_a, vsend.at[0], vrecv.at[pl.ds(0, 1)])
        square = plane_sum(co, SUM_PLANES[1], square, slots_b, vsend.at[1], vrecv.at[pl.ds(1, 1)])
        square = jnp.full((8, 128), jnp.sum(square), f32)
    squares_out[...] = square
    rest_of = rows_out.at[pl.ds(0, size - 1)]
    pltpu.make_async_copy(rest_of, rest_of, xrecv.at[0]).wait()
    for copy in copies:
        copy.wait_send()


def scatter(partials, before=None):
    size = min(4, DIMS[2]) * DIMS[3]
    with_total = before is not None
    planes = [DIMS[a] * DIMS[b] for a, b in SUM_PLANES]
    return pl.pallas_call(
        functools.partial(scatter_kernel, with_total),
        out_shape=[
            jax.ShapeDtypeStruct((size, T, -(-2 * (CH // size) // 8) * 8, CL), f32),
            jax.ShapeDtypeStruct((T, CH, CL), f32),
            jax.ShapeDtypeStruct((8, 128), f32),
        ],
        in_specs=[pl.BlockSpec(memory_space=pltpu.HBM)] * 3 + [pl.BlockSpec(memory_space=pltpu.VMEM)] * with_total,
        out_specs=[pl.BlockSpec(memory_space=pltpu.VMEM)] * 3,
        scratch_shapes=[s for i in range(3) for s in scatter_scratch(ORDERS[i][::-1])]
        + [
            pltpu.VMEM((3, T, CH, CL), f32),
            pltpu.VMEM((size, T, -(-2 * (CH // size) // 8) * 8, CL), f32),
            pltpu.SemaphoreType.DMA((size,)),
            pltpu.SemaphoreType.DMA((1,)),
        ]
        + [
            pltpu.VMEM((planes[0], 8, 128), f32),
            pltpu.VMEM((planes[1], 8, 128), f32),
            pltpu.SemaphoreType.DMA((2, max(planes))),
            pltpu.SemaphoreType.DMA((2,)),
        ]
        * with_total,
        compiler_params=pltpu.CompilerParams(collective_id=3 if with_total else 2, has_side_effects=True, vmem_limit_bytes=62 * 2**20),
        name="scatter",
    )(*partials, *([before] if with_total else []))

FB = 512
NJ = FB // CL
RC = 256
EPS = 1e-6


def dot(a, b):
    return jnp.dot(a, b, preferred_element_type=f32)


def dot_nt(a, b):
    return lax.dot_general(a, b, (((1,), (1,)), ((), ())), preferred_element_type=f32)


def block_of(ref, j):
    return ref[0, :, j].reshape(-1, CL)


def parts(gate, up, dhid):
    s = jax.nn.sigmoid(gate)
    silu = gate * s
    wide = dhid.astype(bf16).astype(f32)
    hid = (silu * up).astype(bf16)
    dup = (wide * silu).astype(bf16)
    dgate = (wide * up * (s + silu * (1.0 - s))).astype(bf16)
    return hid, dup, dgate


def dhid_of(dh, wd_ref, j):
    return sum(dot_nt(dh[:, t * CL : (t + 1) * CL], wd_ref[t, pl.ds(j * CL, CL), :]) for t in range(T))


def rows_of(i, n=RC):
    return pl.ds(pl.multiple_of(i * n, n), n)


def normed(h):
    wide = h.astype(f32)
    scale = lax.rsqrt(jnp.mean(wide**2, -1, keepdims=True) + EPS)
    return (wide * scale).astype(bf16)


def weight_gradients(at_ref, dh_ref, dgate, dup, hid_t, pg_ref, pu_ref, pd_ref):
    d = at_ref.shape[0]
    mc = 16 * CH
    for src, dst in ((dgate, pg_ref), (dup, pu_ref)):
        for m in range(d // mc):
            for j in range(NJ):
                value = dot(at_ref[pl.ds(m * mc, mc), :], src[:, pl.ds(j * CL, CL)])
                dst[0, pl.ds(m * 16, 16), j] = value.reshape(16, CH, CL).astype(bf16)
    for j in range(NJ):
        value = dot(hid_t[pl.ds(j * CL, CL), :], dh_ref[...]).astype(bf16)
        for t in range(T):
            pd_ref[t, pl.ds(j * CL, CL), :] = value[:, t * CL : (t + 1) * CL]


def first_kernel(x_ref, wg_ref, wu_ref, wd_ref, gate_ref, up_ref, at_ref, h_ref, a2_ref, a2t_ref, a_s, y_s):
    b = pl.program_id(0)
    n = x_ref.shape[0] // RC

    @pl.when(b == 0)
    def _():
        for i in range(n):
            r = pl.ds(i * RC, RC)
            a = normed(x_ref[r, :])
            a_s[r, :] = a
            at_ref[:, r] = a.T
        y_s[...] = jnp.zeros_like(y_s)

    def chunk(i, _):
        r = rows_of(i)
        hids = []
        for j in range(NJ):
            c = pl.ds(j * CL, CL)
            gate = dot(a_s[r, :], block_of(wg_ref, j))
            up = dot(a_s[r, :], block_of(wu_ref, j))
            gate_ref[0, r, c] = gate
            up_ref[0, r, c] = up
            hids.append((gate * jax.nn.sigmoid(gate) * up).astype(bf16))
        hid = jnp.concatenate(hids, axis=1)
        for t in range(T):
            c = pl.ds(t * CL, CL)
            y_s[r, c] += dot(hid, wd_ref[t])
        return 0

    lax.fori_loop(0, n, chunk, 0)

    @pl.when(b == pl.num_programs(0) - 1)
    def _():
        for i in range(n):
            r = pl.ds(i * RC, RC)
            h = x_ref[r, :] + y_s[r, :].astype(bf16)
            h_ref[r, :] = h
            a2 = normed(h)
            a2_ref[r, :] = a2
            a2t_ref[:, r] = a2.T


def weight_spec():
    nt = 8 // NJ
    return pl.BlockSpec((1, 32, NJ, CH, CL), lambda b: (b // nt, 0, b % nt, 0, 0))


def down_spec():
    return pl.BlockSpec((T, FB, CL), lambda b: (0, b, 0))


def whole(shape):
    return pl.BlockSpec(shape, lambda b: (0,) * len(shape))


PARAMS = dict(vmem_limit_bytes=60 * 2**20, dimension_semantics=("arbitrary",))


def cost(matmuls, bytes_accessed):
    return pl.CostEstimate(flops=matmuls * 2 * 1024 * 768 * 6144, bytes_accessed=bytes_accessed, transcendentals=1024 * 6144)


def first(x, wg, wu, wd):
    tokens, d = x.shape
    ff = wd.shape[1]
    nb = ff // FB
    return pl.pallas_call(
        first_kernel,
        grid=(nb,),
        in_specs=[whole((tokens, d)), weight_spec(), weight_spec(), down_spec()],
        out_specs=[
            pl.BlockSpec((1, tokens, FB), lambda b: (b, 0, 0)),
            pl.BlockSpec((1, tokens, FB), lambda b: (b, 0, 0)),
            whole((d, tokens)),
            whole((tokens, d)),
            whole((tokens, d)),
            whole((d, tokens)),
        ],
        out_shape=[
            jax.ShapeDtypeStruct((nb, tokens, FB), f32),
            jax.ShapeDtypeStruct((nb, tokens, FB), f32),
            jax.ShapeDtypeStruct((d, tokens), bf16),
            jax.ShapeDtypeStruct((tokens, d), bf16),
            jax.ShapeDtypeStruct((tokens, d), bf16),
            jax.ShapeDtypeStruct((d, tokens), bf16),
        ],
        scratch_shapes=[pltpu.VMEM((tokens, d), bf16), pltpu.VMEM((tokens, d), f32)],
        compiler_params=pltpu.CompilerParams(**PARAMS),
        cost_estimate=cost(3, 80 * 2**20),
        name="first_layer",
    )(x, wg, wu, wd)


def second_kernel(a_ref, at_ref, h_ref, dy_ref, wg_ref, wu_ref, wd_ref, pg_ref, pu_ref, pd_ref, dh_ref, da_s, dgate_s, dup_s, hid_t):
    b = pl.program_id(0)
    n = a_ref.shape[0] // RC

    @pl.when(b == 0)
    def _():
        da_s[...] = jnp.zeros_like(da_s)

    def chunk(i, _):
        r = rows_of(i)
        a = a_ref[r, :]
        dy = dy_ref[r, :]
        da = da_s[r, :]
        for j in range(NJ):
            c = pl.ds(j * CL, CL)
            wg, wu = block_of(wg_ref, j), block_of(wu_ref, j)
            hid, dup, dgate = parts(dot(a, wg), dot(a, wu), dhid_of(dy, wd_ref, j))
            dgate_s[r, c] = dgate
            dup_s[r, c] = dup
            hid_t[c, r] = hid.T
            da += dot_nt(dgate, wg) + dot_nt(dup, wu)
        da_s[r, :] = da
        return 0

    lax.fori_loop(0, n, chunk, 0)
    weight_gradients(at_ref, dy_ref, dgate_s, dup_s, hid_t, pg_ref, pu_ref, pd_ref)

    @pl.when(b == pl.num_programs(0) - 1)
    def _():
        for i in range(n):
            r = pl.ds(i * RC, RC)
            wide = h_ref[r, :].astype(f32)
            da = da_s[r, :].astype(bf16).astype(f32)
            scale = lax.rsqrt(jnp.mean(wide**2, -1, keepdims=True) + EPS)
            inner = jnp.mean(da * wide, -1, keepdims=True)
            dh = da * scale - wide * (inner * scale * scale * scale)
            dh_ref[r, :] = dy_ref[r, :] + dh.astype(bf16)


def second(a, at, h, dy, wg, wu, wd):
    tokens, d = a.shape
    ff = wd.shape[1]
    return pl.pallas_call(
        second_kernel,
        grid=(ff // FB,),
        in_specs=[whole((tokens, d)), whole((d, tokens)), whole((tokens, d)), whole((tokens, d)), weight_spec(), weight_spec(), down_spec()],
        out_specs=[weight_spec(), weight_spec(), down_spec(), whole((tokens, d))],
        out_shape=[
            jax.ShapeDtypeStruct(wg.shape, bf16),
            jax.ShapeDtypeStruct(wg.shape, bf16),
            jax.ShapeDtypeStruct(wd.shape, bf16),
            jax.ShapeDtypeStruct((tokens, d), bf16),
        ],
        scratch_shapes=[pltpu.VMEM((tokens, d), f32), pltpu.VMEM((tokens, FB), bf16), pltpu.VMEM((tokens, FB), bf16), pltpu.VMEM((FB, tokens), bf16)],
        compiler_params=pltpu.CompilerParams(**PARAMS),
        cost_estimate=cost(8, 60 * 2**20),
        name="second_layer",
    )(a, at, h, dy, wg, wu, wd)


def third_kernel(gate_ref, up_ref, at_ref, dh_ref, wd_ref, pg_ref, pu_ref, pd_ref, dgate_s, dup_s, hid_t):
    n = dh_ref.shape[0] // RC

    def chunk(i, _):
        r = rows_of(i)
        dh = dh_ref[r, :]
        for j in range(NJ):
            c = pl.ds(j * CL, CL)
            hid, dup, dgate = parts(gate_ref[0, r, c], up_ref[0, r, c], dhid_of(dh, wd_ref, j))
            dgate_s[r, c] = dgate
            dup_s[r, c] = dup
            hid_t[c, r] = hid.T
        return 0

    lax.fori_loop(0, n, chunk, 0)
    weight_gradients(at_ref, dh_ref, dgate_s, dup_s, hid_t, pg_ref, pu_ref, pd_ref)


def third(gate, up, at, dh, wd, like):
    tokens, d = dh.shape
    ff = wd.shape[1]
    return pl.pallas_call(
        third_kernel,
        grid=(ff // FB,),
        in_specs=[
            pl.BlockSpec((1, tokens, FB), lambda b: (b, 0, 0)),
            pl.BlockSpec((1, tokens, FB), lambda b: (b, 0, 0)),
            whole((d, tokens)),
            whole((tokens, d)),
            down_spec(),
        ],
        out_specs=[weight_spec(), weight_spec(), down_spec()],
        out_shape=[jax.ShapeDtypeStruct(like.shape, bf16), jax.ShapeDtypeStruct(like.shape, bf16), jax.ShapeDtypeStruct(wd.shape, bf16)],
        scratch_shapes=[pltpu.VMEM((tokens, FB), bf16), pltpu.VMEM((tokens, FB), bf16), pltpu.VMEM((FB, tokens), bf16)],
        compiler_params=pltpu.CompilerParams(**PARAMS),
        cost_estimate=cost(4, 90 * 2**20),
        name="first_layer_back",
    )(gate, up, at, dh, wd)


def adamw(w, m, v, g):
    m = 0.9 * m + 0.1 * g
    v = 0.95 * v + 0.05 * g * g
    step = m * lax.rsqrt(v + 1e-8) + 0.1 * w
    return (w - 0.02 * step).astype(bf16), m, v


def solution(mesh):
    def step(x, dy, w_gate, w_up, w_down, *moments):
        m, v = moments[:3], moments[3:]
        weights = (w_gate, w_up, w_down)
        layers, per, ff = w_gate.shape
        size = CH // per
        rows = jnp.stack([w_gate, w_up], 1).astype(f32).reshape(layers, 2, per, T, size, CL).transpose(4, 3, 0, 1, 2, 5)
        rows = rows.reshape(size, T, layers * 2 * per, CL)
        rows = jnp.pad(rows, ((0, 0), (0, 0), (0, -rows.shape[2] % 8), (0, 0)))
        down = w_down.reshape(layers, CH, T, CL).transpose(0, 2, 1, 3)
        full = gather(layers, rows, down)
        blocks = (T, 32, 8, CH, CL)
        shapes = (blocks, blocks, (T, 256 * CH, CL))
        first_w, second_w = ([a.reshape(s) for a, s in zip(full[3 * l : 3 * l + 3], shapes)] for l in range(2))
        gate, up, a1t, h1, a2, a2t = first(x[0], *first_w)
        *partial2, dh1 = second(a2, a2t, h1, dy[0], *second_w)
        partial1 = third(gate, up, a1t, dh1, first_w[2], first_w[0])
        cut = (T,) + DIMS + (CH, CL)
        rows2, down2, square2 = scatter([p.reshape(cut) for p in partial2])
        rows1, down1, total = scatter([p.reshape(cut) for p in partial1], square2)

        def rows_of_gradient(got, i):
            return got[:, :, per * i : per * i + per].transpose(2, 1, 0, 3).reshape(per, ff)

        gradients = [jnp.stack([rows_of_gradient(r, i) for r in (rows1, rows2)]) for i in range(2)]
        gradients.append(jnp.stack([d.transpose(1, 0, 2).reshape(CH, T * CL) for d in (down1, down2)]))
        count = 256 * sum(w.size for w in weights)
        factor = jnp.minimum(1.0, 0.5 * lax.rsqrt(total[0, 0] / count + 1e-30))
        new = [adamw(w.astype(f32), m, v, g * factor) for w, m, v, g in zip(weights, m, v, gradients, strict=True)]
        return tuple(one[which] for which in range(3) for one in new)

    states, cut = P(("rep", "dp"), None, None), P(None, "dp", None)
    return jax.shard_map(
        step,
        mesh=mesh,
        in_specs=(states, states) + (cut,) * 9,
        out_specs=(P("rep", "dp", None),) * 9,
        check_vma=False,
    )
```

time: 2240 us -> 627 us (0.28)
  waiting for transfers between devices: 1720 us -> 0 us
  Pallas kernels: 0 us -> 605 us
  matrix products: 388 us -> 0 us
  blocking collectives: 76.9 us -> 0 us
    reduce_scatter x2 -> x0, waiting for transfers between devices: 677 us -> none  [step(): lax.psum_scatter(by_w[name], 'dp', scatter_dimension=0, tiled=True)]
    all_gather x6 -> x0, waiting for transfers between devices: 608 us -> none  [fetched(): lax.all_gather(w[number], 'dp', axis=0, tiled=True)]
    pallas_call x0 -> x6, Pallas kernels: none -> 605 us  [the longest x2 206 us: scatter(): pl.pallas_call(functools.partial(scatter_kernel, with_total), out_shape=[...]
    unnamed x10 -> x0, waiting for transfers between devices: 435 us -> none
    dot_general x15 -> x0, matrix products: 388 us -> none  [the longest x5 154 us: layer(): up = jnp.dot(a, w['w_up'], preferred_element_type=jnp.float32)]
    psum x1 -> x0, blocking collectives: 76.9 us -> none  [step(): squares = lax.psum(sum((jnp.sum(g * g) for g in gradients)), 'dp')]
  transfers between devices with their start and end apart: 9 -> 0, of which waited for: 9 -> 0; matrix products, arithmetic and copies ran while one was open for 13% -> 0% of each run, Pallas kernels for 0% -> 0%
where the time goes in v1:
time: 627 us; the launch traced here: 626 us
  Pallas kernels  605 us (96%)
  local copies, waits for them, and re-layouts  18.1 us (3%)
    pallas_call x2, Pallas kernels, scatter(): pl.pallas_call(functools.partial(scatter_kernel, with_total), out_shape=[...  206 us
    pallas_call x1, Pallas kernels, gather(): pl.pallas_call(functools.partial(gather_kernel, layers), out_shape=[whole...  160 us
    pallas_call x1, Pallas kernels, second(): pl.pallas_call(second_kernel, grid=(ff // FB,), in_specs=[whole((tokens,...  126 us
    pallas_call x1, Pallas kernels, third(): pl.pallas_call(third_kernel, grid=(ff // FB,), in_specs=[pl.BlockSpec((1,...  60.6 us
    pallas_call x1, Pallas kernels, first(): pl.pallas_call(first_kernel, grid=(nb,), in_specs=[whole((tokens, d)), we...  52.6 us

profile of v1, /device:TPU:1, one launch (start us, length us, event | category | flops | bytes accessed | tf_op | source)
XLA Modules:
  0.0 626.2 jit_solution(10794321171170755987)
XLA Ops:
  0.6 0.9 copy.83
  1.5 0.9 stack.18
  2.5 0.9 stack.19
  3.5 159.6 %gather.1 = (bf16[3,4,4,8,2,24,256]{6,5,4,3,2,1,0:T(8,128)(2,1)S(1)}, bf16[3,4,4,8,2,24,256]{6,5,4,3,2,1,0:T(8,128)(2,1)S(1)}, bf16[3,4,4,8,2,24,256]{6,5,4,3,2,...) custom-call(f32[8,3,16,256]{3,2,1,0:T(8,128)S(1)} %pad_convert_fusio, ...), custom_call_target="tpu_custom_call" | custom-call | tf_op jit(solution)/shard_map/gather/pallas_call | solution.py:486
  163.2 3.5 copy-done
  166.7 3.6 copy-done.1
  170.3 52.6 %first_layer.1 = (f32[12,1024,512]{2,1,0:T(8,128)}, f32[12,1024,512]{2,1,0:T(8,128)}, bf16[768,1024]{1,0:T(8,128)(2,1)}, bf16[1024,768]{1,0:T(8,128)(2,1)}, bf16...) custom-call(bf16[1024,768]{1,0:T(8,128)(2,1)} %bitcast.65, bf16[3,32,8,24,256]{4,3,2,1,0:T(8,128)(2,1)} %bitcast.48, ...), custom_call_target="tpu_custom_call" | custom-call | flops 28991029248 | bytes 83886080 | tf_op jit(solution)/shard_map/first_layer/pallas_call | solution.py:704
  222.9 126.0 %second_layer.1 = (bf16[3,32,8,24,256]{4,3,2,1,0:T(8,128)(2,1)}, bf16[3,32,8,24,256]{4,3,2,1,0:T(8,128)(2,1)}, bf16[3,6144,256]{2,1,0:T(8,128)(2,1)}, bf16[1024,768]{1,0:T(8,128)(2,1)}) custom-call(bf16[1024,768]{1,0:T(8,128)(2,1)} %get-tuple-element.40.a_ref, bf16[768,1024]{1,0:T(8,128)(2,1)} %get-tuple-element.41.at_ref, ...), custom_call_target="tpu_custom_call" | custom-call | flops 77309411328 | bytes 62914560 | tf_op jit(solution)/shard_map/second_layer/pallas_call | solution.py:773
  348.9 60.6 %first_layer_back.1 = (bf16[3,32,8,24,256]{4,3,2,1,0:T(8,128)(2,1)}, bf16[3,32,8,24,256]{4,3,2,1,0:T(8,128)(2,1)}, bf16[3,6144,256]{2,1,0:T(8,128)(2,1)}) custom-call(f32[12,1024,512]{2,1,0:T(8,128)} %get-tuple-element.37.gate_ref, f32[12,1024,512]{2,1,0:T(8,128)} %get-tuple-element.38.up_ref, bf16[768,1024]{1,0:T(8,128)(2,1)} %get-tuple-element.39.at_ref, ...), custom_call_target="tpu_custom_call" | custom-call | flops 38654705664 | bytes 94371840 | tf_op jit(solution)/shard_map/first_layer_back/pallas_call | solution.py:812
  409.5 96.9 %scatter.2 = (f32[8,3,8,256]{3,2,1,0:T(8,128)}, f32[3,24,256]{2,1,0:T(8,128)}, f32[8,128]{1,0:T(8,128)}) custom-call(bf16[3,4,4,8,2,24,256]{6,5,4,3,2,1,0:T(8,128)(2,1)} %bitcast.50, bf16[3,4,4,8,2,24,256]{6,5,4,3,2,1,0:T(8,128)(2,1)} %bitcast.51, bf16[3,4,4,8,2,24,256]{6,5,4,3,2,1,0:T(8,128)(2,1)} %bitcast.52), custom_call_target="tpu_custom_call" | custom-call | tf_op jit(solution)/shard_map/scatter/pallas_call | solution.py:555
  506.6 109.0 %scatter.3 = (f32[8,3,8,256]{3,2,1,0:T(8,128)}, f32[3,24,256]{2,1,0:T(8,128)}, f32[8,128]{1,0:T(8,128)}) custom-call(bf16[3,4,4,8,2,24,256]{6,5,4,3,2,1,0:T(8,128)(2,1)} %bitcast.53, bf16[3,4,4,8,2,24,256]{6,5,4,3,2,1,0:T(8,128)(2,1)} %bitcast.54, bf16[3,4,4,8,2,24,256]{6,5,4,3,2,1,0:T(8,128)(2,1)} %bitcast.55, f32[8,128]{1,0:T(8,128)} %get-tuple-element.53.refs_3_), custom_call_target="tpu_custom_call" | custom-call | tf_op jit(solution)/shard_map/scatter/pallas_call | solution.py:555
  615.6 1.2 slice.17
  617.5 1.1 slice_bitcast_fusion.1
  618.7 0.9 copy.55
  619.6 0.1 stack_reshape.22
  619.7 0.1 stack_reshape.23
  620.0 0.8 fusion.12
  620.8 0.8 fusion.2
  621.7 0.7 copy.57
  622.4 0.7 copy.58
  623.1 0.8 copy.61
  623.9 0.8 copy.59
  624.7 0.8 copy.62
  625.5 0.8 copy.60
  (38 shorter events, 0.5 us)
Async XLA Ops:
  163.2 3.5 copy-start
  166.7 3.6 copy-start.1
  506.4 113.2 %copy-start.12 = (f32[3,24,256]{2,1,0:T(8,128)S(1)}, f32[3,24,256]{2,1,0:T(8,128)}, u32[]{:S(2)}) copy-start(f32[3,24,256]{2,1,0:T(8,128)} %get-tuple-element.58) | copy-start | bytes 221188
  506.4 113.4 %copy-start.5 = (f32[8,3,8,256]{3,2,1,0:T(8,128)S(1)}, f32[8,3,8,256]{3,2,1,0:T(8,128)}, u32[]{:S(2)}) copy-start(f32[8,3,8,256]{3,2,1,0:T(8,128)} %get-tuple-element.55) | copy-start | bytes 589828
  506.5 113.5 %copy-start.2 = (bf16[2,24,768]{2,1,0:T(8,128)(2,1)S(1)}, bf16[2,24,768]{2,1,0:T(8,128)(2,1)}, u32[]{:S(2)}) copy-start(bf16[2,24,768]{2,1,0:T(8,128)(2,1)} %param.15) | copy-start | bytes 221188
  506.5 113.5 %copy-start.10 = (f32[2,24,768]{2,1,0:T(8,128)S(1)}, f32[2,24,768]{2,1,0:T(8,128)}, u32[]{:S(2)}) copy-start(f32[2,24,768]{2,1,0:T(8,128)} %param.21) | copy-start | bytes 442372
  506.5 113.5 %copy-start.11 = (f32[2,24,768]{2,1,0:T(8,128)S(1)}, f32[2,24,768]{2,1,0:T(8,128)}, u32[]{:S(2)}) copy-start(f32[2,24,768]{2,1,0:T(8,128)} %param.18) | copy-start | bytes 442372
  506.5 114.3 %copy-start.3 = (bf16[2,3,6144]{2,0,1:T(2,128)(2,1)S(1)}, bf16[2,3,6144]{2,0,1:T(2,128)(2,1)}, u32[]{:S(2)}) copy-start(bf16[2,3,6144]{2,0,1:T(2,128)(2,1)} %param.13) | copy-start | bytes 221188
  506.5 114.3 %copy-start.4 = (bf16[2,3,6144]{2,0,1:T(2,128)(2,1)S(1)}, bf16[2,3,6144]{2,0,1:T(2,128)(2,1)}, u32[]{:S(2)}) copy-start(bf16[2,3,6144]{2,0,1:T(2,128)(2,1)} %param.14) | copy-start | bytes 221188
  506.5 114.3 %copy-start.6 = (f32[2,3,6144]{2,0,1:T(2,128)S(1)}, f32[2,3,6144]{2,0,1:T(2,128)}, u32[]{:S(2)}) copy-start(f32[2,3,6144]{2,0,1:T(2,128)} %param.19) | copy-start | bytes 442372
  506.5 114.3 %copy-start.7 = (f32[2,3,6144]{2,0,1:T(2,128)S(1)}, f32[2,3,6144]{2,0,1:T(2,128)}, u32[]{:S(2)}) copy-start(f32[2,3,6144]{2,0,1:T(2,128)} %param.16) | copy-start | bytes 442372
  506.5 114.3 %copy-start.8 = (f32[2,3,6144]{2,0,1:T(2,128)S(1)}, f32[2,3,6144]{2,0,1:T(2,128)}, u32[]{:S(2)}) copy-start(f32[2,3,6144]{2,0,1:T(2,128)} %param.20) | copy-start | bytes 442372
  506.6 114.3 %copy-start.9 = (f32[2,3,6144]{2,0,1:T(2,128)S(1)}, f32[2,3,6144]{2,0,1:T(2,128)}, u32[]{:S(2)}) copy-start(f32[2,3,6144]{2,0,1:T(2,128)} %param.17) | copy-start | bytes 442372

commit v2 on v0

v2 whole, which is shorter than its diff:
```python
import functools
import jax
import jax.numpy as jnp
from jax import lax
from jax.experimental import pallas as pl
from jax.experimental.pallas import tpu as pltpu
from jax.sharding import PartitionSpec as P

DIMS = (4, 4, 8, 2)
T = 3
CH, CL, DR, D = 24, 256, 8, 768
CHUNK, PIECE = (CH, CL), (DR, D)
SHAPES = (CHUNK, CHUNK, PIECE)
XYZ = DIMS[:3]
SIZE, PER = 8, 3
ORDERS = ((0, 1, 2), (2, 1, 0), (2, 0, 1))
MATS = range(len(ORDERS))
WAYS = (1, -1)
BOTH = range(2)
f32, bf16 = jnp.float32, jnp.bfloat16
ALL = slice(None)
LANES = CL // 2
LINK = CH * CL * 2 / 46.6e3
HOP = 3.3


def apart(n):
    return range(1, n)


def part(half):
    return 0.5 if half else 1.0


def flat(co):
    r = co[0]
    for n, i in zip(DIMS[1:], co[1:]):
        r = r * n + i
    return r


class Here(list):
    def __init__(self):
        r = lax.axis_index("dp")
        self.index = r
        for n in DIMS[::-1]:
            self.insert(0, lax.rem(r, n))
            r = lax.div(r, n)
        self.pos, self.dev = [], []
        for axis, n in enumerate(DIMS):
            self.pos.append([self[axis]] + [lax.rem(self[axis] + k, n) for k in apart(n)])
            self.dev.append([flat(self[:axis] + [p] + self[axis + 1 :]) for p in self.pos[axis]])
        self.partner = self.dev[3][1]
        half = SIZE // 2
        z = lax.rem(self[2], half)
        base = self.index - z * 2 - self[3]
        self.mine = z * 2 + self[3]
        self.group = [(j, base + j) for j in (lax.rem(self.mine + k, SIZE) for k in apart(SIZE))]


def place(co, axis, by):
    return co.pos[axis][by % DIMS[axis]]


def peer(co, axis, by):
    return co.dev[axis][by % DIMS[axis]]


def axis_peers(co):
    return [co.dev[a][k] for a in MATS for k in apart(DIMS[a])]


def plane_peers(co, axes):
    (i, m), (j, n) = ((co[a], DIMS[a]) for a in axes)
    strides = [flat([int(a == b) for b in range(len(DIMS))]) for a in axes]
    me = i * n + j
    base = co.index - i * strides[0] - j * strides[1]
    others = [lax.rem(me + k, m * n) for k in apart(m * n)]
    return me, [base + lax.div(o, n) * strides[0] + lax.rem(o, n) * strides[1] for o in others]


PLANES = ((2, 3), (0, 1))


def greet(peers):
    barrier = pltpu.get_barrier_semaphore()
    for peer in peers:
        pl.semaphore_signal(barrier, inc=1, device_id={"dp": peer})
    pl.semaphore_wait(barrier, len(peers))


def remote(src, dst, ssem, rsem, device):
    return pltpu.make_async_remote_copy(src_ref=src, dst_ref=dst, send_sem=ssem, recv_sem=rsem, device_id={"dp": device})


def loop(n, body, lo=0):
    def step(i, _):
        body(i)
        return 0

    lax.fori_loop(lo, lo + n, step, 0)


def await_bytes(view, sem):
    pltpu.make_async_copy(view, view, sem).wait()


def upto(n):
    return pl.ds(0, n)


def side(by):
    return (1 - by) // 2


def cut(n, half):
    return ALL if half is ALL else pl.ds(half * (n // 2), n // 2)


(KEEP, SWAP_SEND, SWAP_RECV, RING_SEND, SEND1, RECV1, SEND2, RECV2, SEND3, RECV3), RING_RECV = range(10), 8
SEMS = 18


def far(n):
    return n * n / 8


class Stream:
    def __init__(self, after=()):
        self.ticks, self.after, self.next, self.ready, self.marks = [], after, 0, 0.0, {}

    def add(self, run, axis=-1, load=0.0, travel=0.0, after=()):
        self.ticks.append((run, axis, load, travel, after))

    def mark(self, name):
        self.marks[name] = len(self.ticks)

    def passed(self, name):
        return self.next >= self.marks[name]


def at(ref, sel, core=ALL):
    index = list(sel) + ([] if core is ALL else [core])
    return ref.at[tuple(index)]


def gather_stream(ref, own, order, co, sems, after=()):
    s = Stream(after)
    c = co[3]
    a1, a2, a3 = order
    n1, n2, n3 = (DIMS[a] for a in order)

    def sel(i, j, k):
        out = [0, 0, 0]
        out[a1], out[a2], out[a3] = i, j, k
        return out

    mine = at(ref, co[:3], c)
    keep = lambda: pltpu.make_async_copy(own, mine, sems.at[KEEP])
    block2 = lambda: at(ref, sel(ALL, co[a2], co[a3]), c)

    def block3(k, half=ALL):
        return at(ref, sel(cut(n1, half), ALL, k), c)

    def forward(view):
        remote(view, view, sems.at[SWAP_SEND], sems.at[SWAP_RECV], co.partner).start()

    def spread(source, target, n, axis, i, j):
        for k in apart(n):
            remote(source, target, sems.at[i], sems.at[j], peer(co, axis, k)).start()

    def one():
        keep().start()
        spread(own, mine, n1, a1, SEND1, RECV1)

    def two():
        await_bytes(at(ref, sel(upto(n1 - 1), 0, 0), c), sems.at[RECV1])
        keep().wait()
        spread(block2(), block2(), n2, a2, SEND2, RECV2)

    def ring(step, by):
        half = side(by) if step == n3 // 2 else ALL
        view = block3(place(co, a3, -by * (step - 1)), half)
        came = block3(place(co, a3, -by * step), half)
        return remote(view, view, sems.at[RING_SEND], sems.at[RING_RECV + 2 * step + side(by)], peer(co, a3, by)), came

    def three(step):
        if step == 1:
            await_bytes(at(ref, sel(ALL, upto(n2 - 1), 0), c), sems.at[RECV2])
        for by in WAYS:
            if step > 1:
                ring(step - 1, by)[0].wait_recv()
            if step <= n3 // 2:
                ring(step, by)[0].start()
        if step == 1:
            forward(block3(co[a3]))
        else:
            for by in WAYS:
                forward(ring(step - 1, by)[1])

    def finish():
        half = at(ref, [ALL] * 3, 1 - c)
        await_bytes(half, sems.at[SWAP_RECV])

    def drain():
        half = at(ref, [ALL] * 3, c)
        await_bytes(half, sems.at[SWAP_SEND])
        await_bytes(at(ref, sel(upto(n1 - 1), 0, 0), c), sems.at[SEND1])
        await_bytes(at(ref, sel(ALL, upto(n2 - 1), 0), c), sems.at[SEND2])
        await_bytes(at(ref, sel(ALL, ALL, upto(n3 - 1)), c), sems.at[RING_SEND])

    s.add(one, a1, far(n1) * LINK, HOP + n1 / 8)
    s.add(two, a2, far(n2) * n1 * LINK, HOP + n2 / 8)
    for step in range(1, n3 // 2 + 1):
        s.add(functools.partial(three, step), a3, n1 * n2 * LINK * part(step == n3 // 2), HOP)
    s.add(functools.partial(three, n3 // 2 + 1), travel=2.0)
    s.add(finish)
    s.mark("done")
    s.add(drain)
    s.mark("end")
    return s


def swap_block(partial, other, m, b, co, sems):
    for half in range(2 if m < 2 else 1):
        index = (ALL, ALL, half * 4 + b) if m < 2 else (b,)
        remote(partial.at[index], other.at[index], sems.at[SWAP_SEND], sems.at[SWAP_RECV], co.partner).start()


def scatter_scratch(deep):
    out = []
    for order, shape in zip(ORDERS, SHAPES):
        n2, n3 = DIMS[order[1]], DIMS[order[0]]
        out += [
            pltpu.VMEM((deep,) + XYZ + shape, bf16),
            pltpu.VMEM((deep,) + XYZ + shape, bf16),
            pltpu.VMEM((n3,) + shape, f32),
            pltpu.VMEM((n2, n3) + shape, bf16),
            pltpu.VMEM((2, n2 - 1, n3) + shape, bf16),
            pltpu.VMEM((2, n3 - 1) + shape, bf16),
            pltpu.SemaphoreType.DMA((T + 1, SEMS)),
            pltpu.SemaphoreType.REGULAR((len(WAYS) + 1,)),
        ]
    return out


SCRATCH = 8


def scatter_stream(kept, order, co, scratch, out, stage, swapped, swaps, rings, before):
    other, came1, total, going, came2, came3, sems, free = scratch
    deep = other.shape[0]
    other, came1 = other.at[stage % deep], came1.at[stage % deep]
    came2, came3, sems = came2.at[stage % 2], came3.at[stage % 2], sems.at[stage]
    s = Stream()
    b3, b2, b1 = order
    n1, n2, n3 = (DIMS[a] for a in (b1, b2, b3))
    p1, p2, p3 = (co[a] for a in (b1, b2, b3))
    mid = n1 // 2

    def sel(q, i=ALL, j=ALL):
        out = [0, 0, 0]
        out[b1], out[b2], out[b3] = q, i, j
        return out

    def chunk_sum(refs, q, i):
        return sum(r[tuple(sel(q, i))].astype(f32) for r in refs)

    def sums(q, lo, size, refs):
        def body(i):
            kept[tuple(sel(q, i))] = chunk_sum(refs, q, i).astype(bf16)

        loop(size, body, lo)

    def ring(step, by):
        q = place(co, b1, by * (mid + 1 - step))
        slot = place(co, b1, mid - 1) if by < 0 and step == mid else q
        half = side(by) if step == 1 else ALL
        view, target = at(kept, sel(q, cut(n2, half))), at(came1, sel(slot, cut(n2, half)))
        return remote(view, target, sems.at[RING_SEND], sems.at[RING_RECV + 2 * step + side(by)], peer(co, b1, by))

    def around(step):
        if step == 1 and swapped:
            await_bytes(other, sems.at[SWAP_RECV])
            await_bytes(other, sems.at[SWAP_SEND])
        for by in WAYS:
            q = place(co, b1, by * (mid + 1 - step))
            if step == 1:
                if stage >= deep:
                    pl.semaphore_wait(free.at[1 + side(by)], 1)
                sums(q, side(by) * (n2 // 2), n2 // 2, (kept, other))
            else:
                ring(step - 1, by).wait_recv()
                if step == 2:
                    sums(q, side(by) * (n2 // 2), n2 // 2, (kept, other, came1))
                    sums(q, side(-by) * (n2 // 2), n2 // 2, (kept, other))
                else:
                    sums(q, 0, n2, (kept, other, came1))
            ring(step, by).start()

    def middle():
        for by in WAYS:
            ring(mid, by).wait_recv()
        opposite = place(co, b1, mid)

        def value(i):
            return chunk_sum((kept, other, came1), p1, i) + came1[tuple(sel(opposite, i))].astype(f32)

        def body(i):
            going[i] = value(i).astype(bf16)

        loop(n2, body)
        total[...] = value(p2)
        for k in apart(n2):
            remote(going.at[place(co, b2, k)], came2.at[k - 1], sems.at[SEND2], sems.at[RECV2], peer(co, b2, k)).start()
        if stage + deep < rings:
            for by in WAYS:
                pl.semaphore_signal(free.at[1 + side(-by)], inc=1, device_id={"dp": peer(co, b1, by)})
        if stage + deep < swaps:
            pl.semaphore_signal(free.at[0], inc=1, device_id={"dp": co.partner})

    def release():
        await_bytes(at(came1, sel(upto(n1 - 1))), sems.at[RING_SEND])

    def late():
        await_bytes(came2, sems.at[RECV2])
        await_bytes(came2, sems.at[SEND2])
        value = total[...] + jnp.sum(came2[...].astype(f32), axis=0)
        total[...] = value
        going[p2] = value.astype(bf16)
        for k in apart(n3):
            remote(going.at[p2, place(co, b3, k)], came3.at[k - 1], sems.at[SEND3], sems.at[RECV3], peer(co, b3, k)).start()

    def last():
        await_bytes(came3, sems.at[RECV3])
        value = total[p3] + jnp.sum(came3[...].astype(f32), axis=0)
        out[...] = value.astype(bf16).astype(f32)
        await_bytes(came3, sems.at[SEND3])

    for step in range(1, mid + 1):
        s.add(functools.partial(around, step), b1, n2 * n3 * LINK * part(step == 1), HOP + 0.7)
        s.marks.setdefault("begun", len(s.ticks))
    s.add(middle, b2, far(n2) * n3 * LINK, HOP + n2 / 8, [(p, "end") for p in before])
    s.mark("middle")
    s.add(release)
    s.mark("free")
    s.add(late, b3, far(n3) * LINK, HOP + n3 / 8)
    s.add(last)
    s.mark("end")
    return s


class Plan:
    def __init__(self, streams):
        self.streams, self.busy, self.now, self.slots, self.done = streams, [0.0] * 4, 0.0, [], {}

    def open(self, s):
        return s.next < len(s.ticks) and all(other.passed(name) for other, name in (*s.after, *s.ticks[s.next][-1]))

    def run(self, s):
        run, axis, load, travel, _ = s.ticks[s.next]
        self.slots[-1].append(run)
        begin = max(self.now, self.busy[axis])
        if load:
            self.busy[axis] = begin + load
        s.next += 1
        s.ready = begin + load + travel

    def slot(self, length=0.0):
        self.slots.append([])
        more = True
        while more:
            more = False
            for s in self.streams:
                if self.open(s) and s.ready <= self.now:
                    self.run(s)
                    more = True
        self.now += length

    def need(self, wanted):
        while not all(s.passed(name) for s, name in wanted):
            s = min((s for s in self.streams if self.open(s)), key=lambda s: s.ready)
            self.now = max(self.now, s.ready)
            self.run(s)

    def take(self):
        out, self.slots = self.slots, []
        return out


def run_slot(slots, index, fold=8):
    for lo in range(0, len(slots), fold):
        some = slots[lo : lo + fold]
        if any(some):

            def inner(lo=lo, some=some):
                for i, ticks in enumerate(some):
                    if ticks:

                        @pl.when(index == lo + i)
                        def _(ticks=ticks):
                            for tick in ticks:
                                tick()

            pl.when(lax.div(index, fold) == lo // fold)(inner)

TOKENS = 1024
FB = 512
NJ = FB // CL
NB = 4
RC = 512
NC = TOKENS // RC
END = NC - 1
EPS = 1e-6
NORM = 128
LAST = T * NB - 1
WIDE = (2, 4, 4, 2, 2) + CHUNK


def dot(a, b):
    return jnp.dot(a, b, preferred_element_type=f32)


def dot_nt(a, b):
    return lax.dot_general(a, b, (((1,), (1,)), ((), ())), preferred_element_type=f32)


def odd(b):
    return lax.rem(b, 2)


def rows_of(i, n=RC):
    return pl.ds(pl.multiple_of(i * n, n), n)


def over_rows(body):
    loop(TOKENS // NORM, lambda i: body(rows_of(i, NORM)))


def normed(h):
    wide = h.astype(f32)
    scale = lax.rsqrt(jnp.mean(wide**2, -1, keepdims=True) + EPS)
    return (wide * scale).astype(bf16)


def fetch(refs, b, w, wd, sems):
    out = []
    for m in MATS:
        if m in refs:
            ref = refs[m]
            if m < 2:
                for half in BOTH:
                    out.append(pltpu.make_async_copy(ref.at[:, :, half * 4 + b], w.at[m, :, :, half], sems.at[m, half]))
            else:
                out.append(pltpu.make_async_copy(ref.at[b], wd, sems.at[m, 0]))
    return out


def rows_of_down(wd, j):
    return wd[pl.ds(2 * j, 2)].reshape(CL, D)


def columns_of(w, m, j):
    return w[m, :, :, :, j].reshape(D, CL)


def pieces(device):
    return [(lax.rem(T * device + i, DEVICES), lax.div(T * device + i, DEVICES)) for i in range(T)]


def origins(device):
    return [(lax.div(DEVICES * t + device, T), lax.rem(DEVICES * t + device, T)) for t in range(T)]


def piece_peers(here):
    return [d for d, _ in pieces(here) + origins(here)]


def routes(out, here):
    return [(i, *to) for i, to in enumerate(pieces(here) if out else origins(here))]


def start_pieces(src, dst, here, sems, out):
    for i, device, slot in routes(out, here):

        @pl.when(device != here)
        def _(i=i, device=device, slot=slot):
            remote(src.at[i], dst.at[slot], sems.at[i], sems.at[T + slot], device).start()

        @pl.when(device == here)
        def _(i=i, slot=slot):
            dst[slot] = src[i]


def await_pieces(src, dst, here, sems, out):
    for i, device, _ in routes(out, here):

        @pl.when(device != here)
        def _(i=i):
            await_bytes(src.at[i], sems.at[i])

    for i, device, _ in routes(not out, here):

        @pl.when(device != here)
        def _(i=i):
            await_bytes(dst.at[i], sems.at[T + i])


def parts(gate, up, dhid):
    s = jax.nn.sigmoid(gate)
    silu = gate * s
    wide = dhid.astype(bf16).astype(f32)
    hid = (silu * up).astype(bf16)
    dup = (wide * silu).astype(bf16)
    dgate = (wide * up * (s + silu * (1.0 - s))).astype(bf16)
    return hid, dup, dgate


def weight_gradients(at_s, dh_s, dgate, dup, hid_t, wide, down, slots, b):
    half = D // 2
    for m, src in enumerate((dgate, dup)):
        for i in BOTH:
            for j in range(NJ):
                value = dot(at_s[pl.ds(i * half, half), :], src[:, pl.ds(j * CL, CL)]).reshape((2, 4, 2) + CHUNK).astype(bf16)
                for z in BOTH:
                    wide[slots[j], m, pl.ds(2 * i, 2), :, z * 4 + b] = value[:, :, z]
    for j in range(NJ):
        value = dot(hid_t[pl.ds(j * CL, CL), :], dh_s[...]).reshape((2, 8, 2) + PIECE).astype(bf16)
        for c in BOTH:
            down[slots[c], b, pl.ds(2 * j, 2)] = value[:, :, c]


def gradients_step(co, tensors, buffers, scratch, stage, b, deep):
    wide_s, down_s = buffers
    slot = lax.rem(stage, deep)
    slots = [slot * me + deep * (1 - me) for me in (1 - co[3], co[3])]
    weight_gradients(*tensors, wide_s, down_s, slots, b)

    @pl.when(stage >= deep)
    def _():
        @pl.when(b == 0)
        def _():
            for m in MATS:
                pl.semaphore_wait(scratch[m][SCRATCH - 1].at[0], 1)

    for m in MATS:
        swap_block(wide_s.at[deep, m] if m < 2 else down_s.at[deep], scratch[m][0].at[slot], m, b, co, scratch[m][SCRATCH - 2].at[stage])


def scatter_stage(plan, scatters, co, buffers, scratch, sums, swapped, swaps, rings, deep, start):
    n = len(scatters)
    stage = []
    for m in MATS:
        before = [scatters[n - 1][m]] if n else []
        kept = buffers[0].at[n % deep, m] if m < 2 else buffers[1].at[n % deep]
        stage.append(scatter_stream(kept, ORDERS[m], co, scratch[m], sums(n, m), n, swapped, swaps, rings, before))
        stage[m].ready = start
    scatters.append(stage)
    plan.streams += stage


def forward_kernel(rows_ref, down_ref, x_ref, dy_ref, *refs):
    full, refs = (refs[:3], refs[3:6]), refs[6:]
    gate_ref, up_ref, at_ref, dh_ref, wide_kept, down_kept, *refs = refs
    other_kept, refs = refs[:3], refs[3:]
    sums, dsums, *refs = refs
    scratch = [refs[SCRATCH * m : SCRATCH * (m + 1)] for m in MATS]
    got, wide, chunks, eights, a_s, at_s, h_s, dh_s, acc, dgate_s, dup_s, hid_t, w, wd, held, wide_s, down_s, *refs = refs[SCRATCH * 3 :]
    gsems, wsems, hsems, lsems, xsems, dsems = refs
    co = Here()
    mine, here = co.mine, co.index
    greet(axis_peers(co) + [co.partner] + [device for _, device in co.group] + piece_peers(here))

    stages = 2 * T
    rest = pl.ds(1, stages - 1)

    def swap(j, device, part, i):
        return remote(rows_ref.at[j, part], got.at[mine, part], xsems.at[i], xsems.at[i + 1], device)

    for part, i in ((0, 0), (rest, 2)):
        for j, device in co.group:
            swap(j, device, part, i).start()
        if i == 0:
            start_pieces(down_ref, eights, here, dsems, True)
    loads = [pltpu.make_async_copy(src, dst, lsems.at[i]) for i, (src, dst) in enumerate(((x_ref, h_s), (dy_ref, dh_s)))]
    for copy in loads:
        copy.start()
    got[pl.ds(mine, 1)] = rows_ref[pl.ds(mine, 1)]
    others = got.at[upto(SIZE - 1)]

    def own(n):
        for m in BOTH:
            for j in range(SIZE):
                wide[pl.ds(PER * j, PER), :] = got[j, n, pl.ds(m * PER, PER), :]
            chunks[n, m] = wide[...].astype(bf16)

    await_bytes(others.at[:, 0], xsems.at[1])
    own(0)
    await_pieces(down_ref, eights, here, dsems, True)
    gathers, scatters = [], []
    for n in range(stages):
        after = [(s, "begin") for s in gathers[n - 1]] if n else []
        l, t = n // T, n % T
        stage = [gather_stream(full[l][m].at[t], chunks.at[n, m] if m < 2 else eights.at[t, l], ORDERS[m], co, gsems.at[n, m], after) for m in MATS]
        for s in stage:
            s.marks["begin"] = BEGIN
        gathers.append(stage)
    plan = Plan([s for stage in gathers for s in stage])

    def now():
        for ticks in plan.take():
            for tick in ticks:
                tick()

    def start_scatter():
        scatter_stage(plan, scatters, co, (wide_s, down_s), scratch, lambda n, m: sums.at[n, m] if m < 2 else dsums.at[n], True, T, DEEP, DEEP, plan.now + SETTLE)

    plan.slot(6.0)
    now()
    for copy in loads:
        copy.wait()

    def norm(r):
        a = normed(h_s[r, :])
        a_s[r, :] = a
        at_s[:, r] = a.T
        acc[r, :] = jnp.zeros((NORM, D), f32)

    over_rows(norm)
    put_at = pltpu.make_async_copy(at_s, at_ref, lsems.at[0])
    put_at.start()
    await_bytes(others.at[:, rest], xsems.at[3])
    for n in range(1, stages):
        own(n)
    plan.slot()
    plan.need([(s, "done") for s in gathers[0]])
    now()

    def weights(layer, t, b):
        return fetch(dict(enumerate(ref.at[t] for ref in full[layer])), lax.rem(b, NB), w.at[odd(b)], wd.at[odd(b)], wsems.at[odd(b)])

    def fetch_next(layer, b):
        for copy in weights(layer, lax.div(b, NB), b):
            copy.start()

    def await_block(b):
        for copy in weights(0, 0, b):
            copy.wait()

    fetch_next(0, 0)
    blocks = T * NB
    for b in range(blocks):
        for i in range(NC):
            plan.slot(FIRST_US)
            if i == END and b % NB == NB - 1 and b < LAST:
                plan.need([(s, "done") for s in gathers[b // NB + 1]])
    slots1 = plan.take()

    def put(b, i):
        return [pltpu.make_async_copy(held.at[i, k], ref.at[b, i], hsems.at[i, k]) for k, ref in enumerate((gate_ref, up_ref))]

    def block1(b):
        await_block(b)
        now_w, now_wd = w.at[odd(b)], wd.at[odd(b)]

        def chunk(i):
            run_slot(slots1, b * NC + i)

            @pl.when(b < LAST)
            def _():
                @pl.when(i == lax.div(lax.rem(b, NB), NB - 1) * (END))
                def _():
                    fetch_next(0, b + 1)

            @pl.when(b > 0)
            def _():
                for copy in put(0, i):
                    copy.wait()

            r = rows_of(i)
            hids = []
            for j in range(NJ):
                c = pl.ds(j * CL, CL)
                gate, up = (dot(a_s[r, :], columns_of(now_w, m, j)) for m in BOTH)
                held[i, 0, :, c] = gate
                held[i, 1, :, c] = up
                hids.append((gate * jax.nn.sigmoid(gate) * up).astype(bf16))
            for copy in put(b, i):
                copy.start()
            for j in range(NJ):
                acc[r, :] += dot(hids[j], rows_of_down(now_wd, j))

        loop(NC, chunk)

    loop(blocks, block1)
    plan.slot()
    plan.need([(s, "done") for s in gathers[T]])
    now()
    fetch_next(1, 0)
    put_at.wait()

    def join(r):
        h_s[r, :] += acc[r, :].astype(bf16)
        norm(r)

    over_rows(join)
    for i in range(NC):
        for copy in put(0, i):
            copy.wait()
    plan.slot(3.0)
    now()

    for b in range(blocks):
        if b and b % NB == 0:
            start_scatter()
        for i in range(NC + 1):
            plan.slot(SECOND_US if i < NC else GRADIENTS_US)
            if i == END and b % NB == NB - 1 and b < LAST:
                plan.need([(s, "done") for s in gathers[b // NB + 1 + T]])
            if i == NC and b and b % NB == 0:
                plan.need([(s, "begun") for s in scatters[-1]])
                if b == DEEP * NB:
                    plan.need([(s, "free") for s in scatters[0]])
    slots2 = plan.take()

    def block2(b):
        await_block(b)
        now_w, now_wd = w.at[odd(b)], wd.at[odd(b)]

        def chunk(i):
            run_slot(slots2, b * (NC + 1) + i)

            @pl.when(b < LAST)
            def _():
                @pl.when(i == END)
                def _():
                    fetch_next(1, b + 1)

            r = rows_of(i)
            a = a_s[r, :]
            dy = dh_s[r, :]
            da = acc[r, :]
            for j in range(NJ):
                c = pl.ds(j * CL, CL)
                gate, up = (dot(a, columns_of(now_w, m, j)) for m in BOTH)
                hid, dup, dgate = parts(gate, up, dot_nt(dy, rows_of_down(now_wd, j)))
                dgate_s[r, c] = dgate
                dup_s[r, c] = dup
                hid_t[c, r] = hid.T
            for j in range(NJ):
                c = pl.ds(j * CL, CL)
                da += dot_nt(dgate_s[r, c], columns_of(now_w, 0, j)) + dot_nt(dup_s[r, c], columns_of(now_w, 1, j))
            acc[r, :] = da

        loop(NC, chunk)
        run_slot(slots2, b * (NC + 1) + NC)
        gradients_step(co, (at_s, dh_s, dgate_s, dup_s, hid_t), (wide_s, down_s), scratch, lax.div(b, NB), lax.rem(b, NB), DEEP)

    loop(blocks, block2)

    def norm_back(r):
        h = h_s[r, :].astype(f32)
        da = acc[r, :].astype(bf16).astype(f32)
        scale = lax.rsqrt(jnp.mean(h**2, -1, keepdims=True) + EPS)
        inner = jnp.mean(da * h, -1, keepdims=True)
        dh_s[r, :] += (da * scale - h * (inner * scale * scale * scale)).astype(bf16)

    over_rows(norm_back)
    last = T - 1
    for m in MATS:
        other, sems = scratch[m][0].at[last % DEEP], scratch[m][SCRATCH - 2].at[last]
        await_bytes(other, sems.at[SWAP_RECV])
        await_bytes(other, sems.at[SWAP_SEND])
    outs = [(dh_s, dh_ref), (wide_s.at[last % DEEP], wide_kept), (down_s.at[last % DEEP], down_kept)] + [(scratch[m][0].at[last % DEEP], other_kept[m]) for m in MATS]
    outs = [pltpu.make_async_copy(src, dst, dsems.at[i]) for i, (src, dst) in enumerate(outs)]
    for copy in outs:
        copy.start()
    plan.slot()
    plan.need([(s, "end") for stage in gathers + scatters for s in stage])
    now()
    for copy in outs:
        copy.wait()
    await_bytes(others.at[:, 0], xsems.at[0])
    await_bytes(others.at[:, rest], xsems.at[2])


FIRST_US = 1.5
SECOND_US = 2.5
THIRD_US = 0.9
GRADIENTS_US = 2.7
DEVICES = 256
BEGIN = 3
DEEP = 2
SETTLE = 3.0
VMEM = 67043328


def backward_kernel(down1, gate_ref, up_ref, at_ref, wide_kept, down_kept, *refs):
    other_kept, refs = refs[:3], refs[3:]
    dh_ref, sums1, dsums1, rows_out, down_out, total_out, *refs = refs
    scratch = [refs[SCRATCH * m : SCRATCH * (m + 1)] for m in MATS]
    at_s, dgate_s, dup_s, hid_t, wd, held, wide_s, down_s, sums, dsums, going, *refs = refs[SCRATCH * 3 :]
    slots_a, slots_b, wsems, hsems, lsems, xsems, psems, dsems = refs
    co = Here()
    planes = [plane_peers(co, axes) for axes in PLANES]
    blocks = T * NB
    ins = [(at_ref, at_s), (wide_kept, wide_s.at[0]), (down_kept, down_s.at[0])] + [(other_kept[m], scratch[m][0].at[0]) for m in MATS]
    ins = [pltpu.make_async_copy(src, dst, lsems.at[i]) for i, (src, dst) in enumerate(ins)]

    def down(b):
        return fetch({2: down1.at[lax.div(b, NB)]}, lax.rem(b, NB), (), wd.at[odd(b)], wsems.at[odd(b)])

    def saved(b, i):
        return [pltpu.make_async_copy(ref.at[b, i], held.at[i, k], hsems.at[i, k]) for k, ref in enumerate((gate_ref, up_ref))]

    for copy in ins + down(0) + [copy for i in range(NC) for copy in saved(0, i)]:
        copy.start()
    greet(axis_peers(co) + [co.partner] + [device for _, device in co.group] + planes[0][1] + planes[1][1] + piece_peers(co.index))
    early = T - 1
    for n in range(early):
        dsums[n, 1] = dsums1[n]
        for m in BOTH:
            sums[n, m] = sums1[n, m]
    for copy in ins:
        copy.wait()
    plan, scatters = Plan([]), []

    def start_scatter(swapped, start):
        def out(n, m):
            n += early
            return sums.at[n, m] if m < 2 else dsums.at[n % T, 1 - n // T]

        scatter_stage(plan, scatters, co, (wide_s, down_s), scratch, out, swapped, T + 1, T + 1, T, start)

    start_scatter(False, 0.0)
    for b in range(blocks):
        if b and b % NB == 0:
            start_scatter(True, plan.now + SETTLE)
        for i in range(NC + 1):
            plan.slot(THIRD_US if i < NC else GRADIENTS_US)
            if i == NC and b and b % NB == 0:
                plan.need([(s, "begun") for s in scatters[-1]])
                if b == early * NB:
                    plan.need([(s, "free") for s in scatters[0]])
    slots3 = plan.take()
    start_scatter(True, plan.now + SETTLE)
    plan.slot()
    plan.need([(s, "end") for stage in scatters for s in stage])

    def block3(b):
        for copy in down(b):
            copy.wait()

        @pl.when(b < LAST)
        def _():
            for copy in down(b + 1):
                copy.start()

        def chunk(i):
            run_slot(slots3, b * (NC + 1) + i)
            for copy in saved(b, i):
                copy.wait()
            r = rows_of(i)
            dh = dh_ref[r, :]
            for j in range(NJ):
                c = pl.ds(j * CL, CL)
                hid, dup, dgate = parts(held[i, 0, :, c], held[i, 1, :, c], dot_nt(dh, rows_of_down(wd.at[odd(b)], j)))
                dgate_s[r, c] = dgate
                dup_s[r, c] = dup
                hid_t[c, r] = hid.T

            @pl.when(b < LAST)
            def _():
                for copy in saved(b + 1, i):
                    copy.start()

        loop(NC, chunk)
        run_slot(slots3, b * (NC + 1) + NC)
        gradients_step(co, (at_s, dh_ref, dgate_s, dup_s, hid_t), (wide_s, down_s), scratch, 1 + lax.div(b, NB), lax.rem(b, NB), T)

    loop(blocks, block3)
    for tick in plan.take()[0]:
        tick()
    finish(co, sums, dsums, going, rows_out, down_out, total_out, (slots_a, slots_b), planes, xsems, psems, dsems)


def finish(co, sums, dsums, going, rows_out, down_out, total_out, planes, groups, xsems, psems, dsems):
    mine, here = co.mine, co.index
    stages = sums.shape[0]
    start_pieces(dsums, down_out, here, dsems, False)

    def fill(n):
        for m in BOTH:
            for j in range(SIZE):
                going[j, n, pl.ds(PER * m, PER), :] = sums[n, m, pl.ds(PER * j, PER), :]

    loop(stages, fill)
    copies = [remote(going.at[j], rows_out.at[mine], xsems.at[0], xsems.at[1], device) for j, device in co.group]
    for copy in copies:
        copy.start()
    rows_out[pl.ds(mine, 1)] = going[pl.ds(mine, 1)]
    square = jnp.sum((sums[...] * sums[...]).reshape(-1, 8, CL), axis=0)
    piece = jnp.sum((dsums[...] * dsums[...]).reshape(-1, 8, D), axis=0)
    square = sum(s[:, i : i + LANES] for s in (square, piece) for i in range(0, s.shape[1], LANES))
    for n, (slots, (me, peers)) in enumerate(zip(planes, groups)):
        slots[me] = square
        for device in peers:
            remote(slots.at[me], slots.at[me], psems.at[2 * n], psems.at[2 * n + 1], device).start()
        others = slots.at[upto(len(peers))]
        await_bytes(others, psems.at[2 * n + 1])
        await_bytes(others, psems.at[2 * n])
        square = jnp.sum(slots[...], axis=0)
    total_out[...] = jnp.full(total_out.shape, jnp.sum(square), f32)
    rest = rows_out.at[upto(SIZE - 1)]
    for n in BOTH:
        await_bytes(rest, xsems.at[n])
    await_pieces(dsums, down_out, here, dsems, False)


def hbm():
    return pl.BlockSpec(memory_space=pltpu.HBM)


def vmem():
    return pl.BlockSpec(memory_space=pltpu.VMEM)


TALL, FLAT, BLOCK = (TOKENS, D), (D, TOKENS), (TOKENS, FB)


def forward(rows, down, x, dy):
    stages = 2 * T
    full = [jax.ShapeDtypeStruct((T,) + DIMS + shape, bf16) for shape in SHAPES]
    kept = jax.ShapeDtypeStruct((T * NB, NC, RC, FB), f32)
    partial = [jax.ShapeDtypeStruct(s, bf16) for s in ((2,) + XYZ + CHUNK, XYZ + PIECE)]
    small = [jax.ShapeDtypeStruct(s, f32) for s in ((DEEP, 2) + CHUNK, (DEEP,) + PIECE)]
    return pl.pallas_call(
        forward_kernel,
        out_shape=full * 2 + [kept] * 2 + [jax.ShapeDtypeStruct(s, bf16) for s in (FLAT, TALL)] + partial + [jax.ShapeDtypeStruct(XYZ + s, bf16) for s in SHAPES] + small,
        in_specs=[vmem(), vmem(), hbm(), hbm()],
        out_specs=[hbm()] * 15 + [vmem()] * 2,
        scratch_shapes=scatter_scratch(DEEP)
        + [
            pltpu.VMEM(rows.shape, f32),
            pltpu.VMEM(CHUNK, f32),
            pltpu.VMEM((stages, 2) + CHUNK, bf16),
            pltpu.VMEM((T, 2) + PIECE, bf16),
            pltpu.VMEM(TALL, bf16),
            pltpu.VMEM(FLAT, bf16),
            pltpu.VMEM(TALL, bf16),
            pltpu.VMEM(TALL, bf16),
            pltpu.VMEM(TALL, f32),
            pltpu.VMEM(BLOCK, bf16),
            pltpu.VMEM(BLOCK, bf16),
            pltpu.VMEM(BLOCK[::-1], bf16),
            pltpu.VMEM((2,) + WIDE, bf16),
            pltpu.VMEM((2,) + DIMS[1:] + PIECE, bf16),
            pltpu.VMEM((NC, 2, RC, FB), f32),
            pltpu.VMEM((DEEP + 1, 2) + XYZ + CHUNK, bf16),
            pltpu.VMEM((DEEP + 1,) + XYZ + PIECE, bf16),
        ]
        + [pltpu.SemaphoreType.DMA(s) for s in ((stages, 3, SEMS), (2, 3, 2), (NC, 2), (2,), (4,), (stages,))],
        compiler_params=pltpu.CompilerParams(collective_id=1, has_side_effects=True, vmem_limit_bytes=VMEM),
        name="forward",
    )(rows, down, x, dy)


def backward(down1, kept, at, partial, dh, sums, shape):
    planes = (16, 8, LANES)
    return pl.pallas_call(
        backward_kernel,
        out_shape=[jax.ShapeDtypeStruct(s, f32) for s in (shape, (T, 2) + PIECE, (8, LANES))],
        in_specs=[hbm()] * 9 + [vmem()] * 3,
        out_specs=[vmem()] * 3,
        scratch_shapes=scatter_scratch(T)
        + [
            pltpu.VMEM(FLAT, bf16),
            pltpu.VMEM(BLOCK, bf16),
            pltpu.VMEM(BLOCK, bf16),
            pltpu.VMEM(BLOCK[::-1], bf16),
            pltpu.VMEM((2,) + DIMS[1:] + PIECE, bf16),
            pltpu.VMEM((NC, 2, RC, FB), f32),
            pltpu.VMEM((T + 1, 2) + XYZ + CHUNK, bf16),
            pltpu.VMEM((T + 1,) + XYZ + PIECE, bf16),
        ]
        + [pltpu.VMEM(s, f32) for s in ((2 * T, 2) + CHUNK, (T, 2) + PIECE, shape, planes, planes)]
        + [pltpu.SemaphoreType.DMA(s) for s in ((2, 3, 2), (NC, 2), (2 * T,), (4,), (4,), (2 * T,))],
        compiler_params=pltpu.CompilerParams(collective_id=2, has_side_effects=True, vmem_limit_bytes=VMEM),
        name="backward",
    )(down1, *kept, at, *partial, dh, *sums)


def adamw(w, m, v, g):
    m = 0.9 * m + 0.1 * g
    v = 0.95 * v + 0.05 * g * g
    step = m * lax.rsqrt(v + 1e-8) + 0.1 * w
    return (w - 0.02 * step).astype(bf16), m, v


def solution(mesh):
    def step(x, dy, w_gate, w_up, w_down, *moments):
        m, v = moments[:3], moments[3:]
        weights = (w_gate, w_up, w_down)
        rows = jnp.stack([w_gate, w_up], 1).reshape(2, 2 * PER, T, SIZE, CL).transpose(3, 0, 2, 1, 4).reshape(SIZE, 2 * T, 2 * PER, CL)
        rows = jnp.pad(rows.astype(f32), ((0, 0), (0, 0), (0, 2), (0, 0)))
        down = w_down.reshape((2, T) + PIECE).transpose(1, 0, 2, 3)
        *full, gate, up, at, dh, wide, narrow, other0, other1, other2, sums, dsums = forward(rows, down, x[0], dy[0])
        rows, down, total = backward(full[2], (gate, up), at, (wide, narrow, other0, other1, other2), dh, (sums, dsums), rows.shape)
        rows = rows[:, :, : 2 * PER].reshape(SIZE, 2, T, 2, PER, CL).transpose(3, 1, 4, 2, 0, 5)[:, ::-1].reshape((2,) + w_gate.shape)
        down = down.transpose(1, 0, 2, 3).reshape(w_down.shape)
        gradients = (rows[0], rows[1], down)
        count = 256 * sum(w.size for w in weights)
        factor = jnp.minimum(1.0, 0.5 * lax.rsqrt(total[0, 0] / count + 1e-30))
        new = [adamw(w.astype(f32), m, v, g * factor) for w, m, v, g in zip(weights, m, v, gradients, strict=True)]
        return tuple(one[which] for which in range(3) for one in new)

    states, cut = P(("rep", "dp"), None, None), P(None, "dp", None)
    return jax.shard_map(
        step,
        mesh=mesh,
        in_specs=(states, states) + (cut,) * 9,
        out_specs=(P("rep", "dp", None),) * 9,
        check_vma=False,
    )
```

time: 2240 us -> 434 us (0.19)
  waiting for transfers between devices: 1720 us -> 0 us
  Pallas kernels: 0 us -> 421 us
  matrix products: 388 us -> 0 us
  blocking collectives: 76.9 us -> 0 us
    reduce_scatter x2 -> x0, waiting for transfers between devices: 677 us -> none  [step(): lax.psum_scatter(by_w[name], 'dp', scatter_dimension=0, tiled=True)]
    all_gather x6 -> x0, waiting for transfers between devices: 608 us -> none  [fetched(): lax.all_gather(w[number], 'dp', axis=0, tiled=True)]
    unnamed x10 -> x0, waiting for transfers between devices: 435 us -> none
    pallas_call x0 -> x2, Pallas kernels: none -> 421 us  [the longest x1 279 us: forward(): pl.pallas_call(forward_kernel, out_shape=full * 2 + [kept] * 2 + [jax.Sha...]
    dot_general x15 -> x0, matrix products: 388 us -> none  [the longest x5 154 us: layer(): up = jnp.dot(a, w['w_up'], preferred_element_type=jnp.float32)]
    psum x1 -> x0, blocking collectives: 76.9 us -> none  [step(): squares = lax.psum(sum((jnp.sum(g * g) for g in gradients)), 'dp')]
  transfers between devices with their start and end apart: 9 -> 0, of which waited for: 9 -> 0; matrix products, arithmetic and copies ran while one was open for 13% -> 0% of each run, Pallas kernels for 0% -> 0%
where the time goes in v2:
time: 434 us; the launch traced here: 433 us
  Pallas kernels  421 us (97%)
  other arithmetic  5.81 us (1%)
  local copies, waits for them, and re-layouts  4.47 us (1%)
    pallas_call x1, Pallas kernels, forward(): pl.pallas_call(forward_kernel, out_shape=full * 2 + [kept] * 2 + [jax.Sha...  279 us
    pallas_call x1, Pallas kernels, backward(): pl.pallas_call(backward_kernel, out_shape=[jax.ShapeDtypeStruct(s, f32) f...  142 us

profile of v2, /device:TPU:1, one launch (start us, length us, event | category | flops | bytes accessed | tf_op | source)
XLA Modules:
  0.0 433.2 jit_solution(18028770336107096653)
XLA Ops:
  0.6 1.5 copy_bitcast_fusion.down_ref
  2.2 1.1 pad_maximum_fusion
  3.3 0.1 convert_element_type.31
  3.5 0.8 pad_convert_fusion.rows_ref
  4.3 279.5 %forward.1 = (bf16[3,4,4,8,2,24,256]{6,5,4,3,2,1,0:T(8,128)(2,1)}, bf16[3,4,4,8,2,24,256]{6,5,4,3,2,1,0:T(8,128)(2,1)}, bf16[3,4,4,8,2,8,768]{6,5,4,3,2,1,0:T(8,...) custom-call(f32[8,6,8,256]{3,2,1,0:T(8,128)} %pad_convert_fusion.row, ...), custom_call_target="tpu_custom_call" | custom-call | tf_op jit(solution)/shard_map/forward/pallas_call | solution.py:937
  283.7 142.0 %backward.1 = (f32[8,6,8,256]{3,2,1,0:T(8,128)}, f32[3,2,8,768]{3,2,1,0:T(8,128)}, f32[8,128]{1,0:T(8,128)}) custom-call(bf16[3,4,4,8,2,8,768]{6,5,4,3,2,1,0:T(8,128)(2,1)} %get-tuple-element.24.down1, f32[12,2,512,512]{3,2,1,0:T(8,128)} %get-tuple-element.25.gate_ref, f32[12,2,512,512]{3,2,1,0:T(8,128)} %get-tuple-element.26.up_ref, ...), custom_call_target="tpu_custom_call" | custom-call | tf_op jit(solution)/shard_map/backward/pallas_call | solution.py:970
  425.7 0.0 copy-start.6
  425.7 0.0 copy-start.7
  425.7 0.0 copy-start.8
  425.7 0.0 copy-start
  425.7 0.0 copy-start.2
  425.8 0.0 copy-start.3
  425.8 0.0 copy-start.1
  425.8 0.0 copy-start.4
  425.8 0.0 copy-start.5
  425.8 1.3 slice.23
  427.8 1.2 copy.29
  429.1 0.1 mul.125
  429.2 0.1 mul.115
  429.3 1.6 fusion.6
  431.0 1.1 fusion.11
  432.1 0.0 copy-done.1
  432.1 0.0 copy-done.5
  432.1 1.1 fusion.12
  (12 shorter events, 0.1 us)
Async XLA Ops:
  425.7 3.6 copy-start.6
  425.7 3.6 copy-start.7
  425.7 3.6 copy-start.8
  425.7 5.3 %copy-start = (bf16[2,3,6144]{2,0,1:T(2,128)(2,1)S(1)}, bf16[2,3,6144]{2,0,1:T(2,128)(2,1)}, u32[]{:S(2)}) copy-start(bf16[2,3,6144]{2,0,1:T(2,128)(2,1)} %param.13) | copy-start | bytes 221188
  425.7 5.3 %copy-start.2 = (f32[2,3,6144]{2,0,1:T(2,128)S(1)}, f32[2,3,6144]{2,0,1:T(2,128)}, u32[]{:S(2)}) copy-start(f32[2,3,6144]{2,0,1:T(2,128)} %param.19) | copy-start | bytes 442372
  425.8 5.2 %copy-start.3 = (f32[2,3,6144]{2,0,1:T(2,128)S(1)}, f32[2,3,6144]{2,0,1:T(2,128)}, u32[]{:S(2)}) copy-start(f32[2,3,6144]{2,0,1:T(2,128)} %param.16) | copy-start | bytes 442372
  425.8 6.3 %copy-start.1 = (bf16[2,3,6144]{2,0,1:T(2,128)(2,1)S(1)}, bf16[2,3,6144]{2,0,1:T(2,128)(2,1)}, u32[]{:S(2)}) copy-start(bf16[2,3,6144]{2,0,1:T(2,128)(2,1)} %param.14) | copy-start | bytes 221188
  425.8 6.3 %copy-start.4 = (f32[2,3,6144]{2,0,1:T(2,128)S(1)}, f32[2,3,6144]{2,0,1:T(2,128)}, u32[]{:S(2)}) copy-start(f32[2,3,6144]{2,0,1:T(2,128)} %param.20) | copy-start | bytes 442372
  425.8 6.3 %copy-start.5 = (f32[2,3,6144]{2,0,1:T(2,128)S(1)}, f32[2,3,6144]{2,0,1:T(2,128)}, u32[]{:S(2)}) copy-start(f32[2,3,6144]{2,0,1:T(2,128)} %param.17) | copy-start | bytes 442372

commit v3 on v2

--- a/solution.py
+++ b/solution.py
@@ -21,6 +21,7 @@
 ALL = slice(None)
 LANES = CL // 2
 LINK = CH * CL * 2 / 46.6e3
+TICK = 0.2
 HOP = 3.3
 
 
@@ -117,8 +118,9 @@
     return ALL if half is ALL else pl.ds(half * (n // 2), n // 2)
 
 
-(KEEP, SWAP_SEND, SWAP_RECV, RING_SEND, SEND1, RECV1, SEND2, RECV2, SEND3, RECV3), RING_RECV = range(10), 8
-SEMS = 18
+(KEEP, SWAP_SEND, SWAP_RECV, RING_SEND, SEND1, RECV1, SEND2, RECV2), RING_RECV = range(8), 8
+SEND3, RECV3 = SEND1, RECV1
+SEMS = 16
 
 
 def far(n):
@@ -144,7 +146,7 @@
     return ref.at[tuple(index)]
 
 
-def gather_stream(ref, own, order, co, sems, after=()):
+def gather_stream(ref, own, order, co, sems, after, ready):
     s = Stream(after)
     c = co[3]
     a1, a2, a3 = order
@@ -170,6 +172,7 @@
             remote(source, target, sems.at[i], sems.at[j], peer(co, axis, k)).start()
 
     def one():
+        ready()
         keep().start()
         spread(own, mine, n1, a1, SEND1, RECV1)
 
@@ -182,7 +185,7 @@
         half = side(by) if step == n3 // 2 else ALL
         view = block3(place(co, a3, -by * (step - 1)), half)
         came = block3(place(co, a3, -by * step), half)
-        return remote(view, view, sems.at[RING_SEND], sems.at[RING_RECV + 2 * step + side(by)], peer(co, a3, by)), came
+        return remote(view, view, sems.at[RING_SEND], sems.at[RING_RECV + 2 * step - 1 - side(by)], peer(co, a3, by)), came
 
     def three(step):
         if step == 1:
@@ -227,7 +230,7 @@
         remote(partial.at[index], other.at[index], sems.at[SWAP_SEND], sems.at[SWAP_RECV], co.partner).start()
 
 
-def scatter_scratch(deep):
+def scatter_scratch(deep, stages):
     out = []
     for order, shape in zip(ORDERS, SHAPES):
         n2, n3 = DIMS[order[1]], DIMS[order[0]]
@@ -238,7 +241,7 @@
             pltpu.VMEM((n2, n3) + shape, bf16),
             pltpu.VMEM((2, n2 - 1, n3) + shape, bf16),
             pltpu.VMEM((2, n3 - 1) + shape, bf16),
-            pltpu.SemaphoreType.DMA((T + 1, SEMS)),
+            pltpu.SemaphoreType.DMA((stages, SEMS)),
             pltpu.SemaphoreType.REGULAR((len(WAYS) + 1,)),
         ]
     return out
@@ -277,7 +280,7 @@
         slot = place(co, b1, mid - 1) if by < 0 and step == mid else q
         half = side(by) if step == 1 else ALL
         view, target = at(kept, sel(q, cut(n2, half))), at(came1, sel(slot, cut(n2, half)))
-        return remote(view, target, sems.at[RING_SEND], sems.at[RING_RECV + 2 * step + side(by)], peer(co, b1, by))
+        return remote(view, target, sems.at[RING_SEND], sems.at[RING_RECV + 2 * step - 1 - side(by)], peer(co, b1, by))
 
     def around(step):
         if step == 1 and swapped:
@@ -360,6 +363,7 @@
     def run(self, s):
         run, axis, load, travel, _ = s.ticks[s.next]
         self.slots[-1].append(run)
+        self.now += TICK
         begin = max(self.now, self.busy[axis])
         if load:
             self.busy[axis] = begin + load
@@ -388,6 +392,10 @@
         return out
 
 
+def only(slots, step, where):
+    return [ticks if q % step in where else () for q, ticks in enumerate(slots)]
+
+
 def run_slot(slots, index, fold=8):
     for lo in range(0, len(slots), fold):
         some = slots[lo : lo + fold]
@@ -412,7 +420,7 @@
 NC = TOKENS // RC
 END = NC - 1
 EPS = 1e-6
-NORM = 128
+NORM = 256
 LAST = T * NB - 1
 WIDE = (2, 4, 4, 2, 2) + CHUNK
 
@@ -480,16 +488,16 @@
     return [(i, *to) for i, to in enumerate(pieces(here) if out else origins(here))]
 
 
-def start_pieces(src, dst, here, sems, out):
-    for i, device, slot in routes(out, here):
-
-        @pl.when(device != here)
-        def _(i=i, device=device, slot=slot):
-            remote(src.at[i], dst.at[slot], sems.at[i], sems.at[T + slot], device).start()
-
-        @pl.when(device == here)
-        def _(i=i, slot=slot):
-            dst[slot] = src[i]
+def start_piece(src, dst, here, sems, route):
+    i, device, slot = route
+
+    @pl.when(device != here)
+    def _():
+        remote(src.at[i], dst.at[slot], sems.at[i], sems.at[T + slot], device).start()
+
+    @pl.when(device == here)
+    def _():
+        dst[slot] = src[i]
 
 
 def await_pieces(src, dst, here, sems, out):
@@ -516,7 +524,7 @@
     return hid, dup, dgate
 
 
-def weight_gradients(at_s, dh_s, dgate, dup, hid_t, wide, down, slots, b):
+def weight_gradients(at_s, dh_s, dgate, dup, hid_t, wide, down, slots, b, between):
     half = D // 2
     for m, src in enumerate((dgate, dup)):
         for i in BOTH:
@@ -524,17 +532,18 @@
                 value = dot(at_s[pl.ds(i * half, half), :], src[:, pl.ds(j * CL, CL)]).reshape((2, 4, 2) + CHUNK).astype(bf16)
                 for z in BOTH:
                     wide[slots[j], m, pl.ds(2 * i, 2), :, z * 4 + b] = value[:, :, z]
+    between()
     for j in range(NJ):
         value = dot(hid_t[pl.ds(j * CL, CL), :], dh_s[...]).reshape((2, 8, 2) + PIECE).astype(bf16)
         for c in BOTH:
             down[slots[c], b, pl.ds(2 * j, 2)] = value[:, :, c]
 
 
-def gradients_step(co, tensors, buffers, scratch, stage, b, deep):
+def gradients_step(co, tensors, buffers, scratch, stage, b, deep, between):
     wide_s, down_s = buffers
     slot = lax.rem(stage, deep)
     slots = [slot * me + deep * (1 - me) for me in (1 - co[3], co[3])]
-    weight_gradients(*tensors, wide_s, down_s, slots, b)
+    weight_gradients(*tensors, wide_s, down_s, slots, b, between)
 
     @pl.when(stage >= deep)
     def _():
@@ -581,7 +590,8 @@
         for j, device in co.group:
             swap(j, device, part, i).start()
         if i == 0:
-            start_pieces(down_ref, eights, here, dsems, True)
+            for route in routes(True, here):
+                start_piece(down_ref, eights, here, dsems, route)
     loads = [pltpu.make_async_copy(src, dst, lsems.at[i]) for i, (src, dst) in enumerate(((x_ref, h_s), (dy_ref, dh_s)))]
     for copy in loads:
         copy.start()
@@ -596,16 +606,20 @@
 
     await_bytes(others.at[:, 0], xsems.at[1])
     own(0)
-    await_pieces(down_ref, eights, here, dsems, True)
     gathers, scatters = [], []
     for n in range(stages):
         after = [(s, "begin") for s in gathers[n - 1]] if n else []
         l, t = n // T, n % T
-        stage = [gather_stream(full[l][m].at[t], chunks.at[n, m] if m < 2 else eights.at[t, l], ORDERS[m], co, gsems.at[n, m], after) for m in MATS]
+        stage = []
+        for m in MATS:
+            chunk = chunks.at[n, m] if m < 2 else eights.at[t, l]
+            ready = (lambda: await_pieces(down_ref, eights, here, dsems, True)) if m == 2 and n == 0 else lambda: ()
+            stage.append(gather_stream(full[l][m].at[t], chunk, ORDERS[m], co, gsems.at[n, m], after, ready))
         for s in stage:
-            s.marks["begin"] = BEGIN
+            s.marks["begin"] = GATES[n]
         gathers.append(stage)
-    plan = Plan([s for stage in gathers for s in stage])
+    soon, *later = gathers
+    plan = Plan(list(soon))
 
     def now():
         for ticks in plan.take():
@@ -630,8 +644,9 @@
     put_at = pltpu.make_async_copy(at_s, at_ref, lsems.at[0])
     put_at.start()
     await_bytes(others.at[:, rest], xsems.at[3])
-    for n in range(1, stages):
+    for n in apart(stages):
         own(n)
+    plan.streams += [s for stage in later for s in stage]
     plan.slot()
     plan.need([(s, "done") for s in gathers[0]])
     now()
@@ -713,7 +728,7 @@
     for b in range(blocks):
         if b and b % NB == 0:
             start_scatter()
-        for i in range(NC + 1):
+        for i in range(SLOTS):
             plan.slot(SECOND_US if i < NC else GRADIENTS_US)
             if i == END and b % NB == NB - 1 and b < LAST:
                 plan.need([(s, "done") for s in gathers[b // NB + 1 + T]])
@@ -728,7 +743,7 @@
         now_w, now_wd = w.at[odd(b)], wd.at[odd(b)]
 
         def chunk(i):
-            run_slot(slots2, b * (NC + 1) + i)
+            run_slot(only(slots2, SLOTS, range(NC)), b * SLOTS + i)
 
             @pl.when(b < LAST)
             def _():
@@ -753,8 +768,8 @@
             acc[r, :] = da
 
         loop(NC, chunk)
-        run_slot(slots2, b * (NC + 1) + NC)
-        gradients_step(co, (at_s, dh_s, dgate_s, dup_s, hid_t), (wide_s, down_s), scratch, lax.div(b, NB), lax.rem(b, NB), DEEP)
+        run_slot(only(slots2, SLOTS, [NC]), b * SLOTS + NC)
+        gradients_step(co, (at_s, dh_s, dgate_s, dup_s, hid_t), (wide_s, down_s), scratch, lax.div(b, NB), lax.rem(b, NB), DEEP, lambda: run_slot(only(slots2, SLOTS, [NC + 1]), b * SLOTS + NC + 1))
 
     loop(blocks, block2)
 
@@ -766,7 +781,7 @@
         dh_s[r, :] += (da * scale - h * (inner * scale * scale * scale)).astype(bf16)
 
     over_rows(norm_back)
-    last = T - 1
+    last = DEEP
     for m in MATS:
         other, sems = scratch[m][0].at[last % DEEP], scratch[m][SCRATCH - 2].at[last]
         await_bytes(other, sems.at[SWAP_RECV])
@@ -787,11 +802,13 @@
 FIRST_US = 1.5
 SECOND_US = 2.5
 THIRD_US = 0.9
-GRADIENTS_US = 2.7
+GRADIENTS_US = 1.35
+SLOTS = NC + 2
 DEVICES = 256
-BEGIN = 3
+GATES = (1, 2, 1, 4, 4, 2)
 DEEP = 2
-SETTLE = 3.0
+LATE = T + 1
+SETTLE = 2.0
 VMEM = 67043328
 
 
@@ -800,7 +817,7 @@
     dh_ref, sums1, dsums1, rows_out, down_out, total_out, *refs = refs
     scratch = [refs[SCRATCH * m : SCRATCH * (m + 1)] for m in MATS]
     at_s, dgate_s, dup_s, hid_t, wd, held, wide_s, down_s, sums, dsums, going, *refs = refs[SCRATCH * 3 :]
-    slots_a, slots_b, wsems, hsems, lsems, xsems, psems, dsems = refs
+    slots_a, slots_b, squares, wsems, hsems, lsems, xsems, psems, dsems = refs
     co = Here()
     planes = [plane_peers(co, axes) for axes in PLANES]
     blocks = T * NB
@@ -816,27 +833,48 @@
     for copy in ins + down(0) + [copy for i in range(NC) for copy in saved(0, i)]:
         copy.start()
     greet(axis_peers(co) + [co.partner] + [device for _, device in co.group] + planes[0][1] + planes[1][1] + piece_peers(co.index))
-    early = T - 1
+    early = DEEP
+    way = routes(False, co.index)
+
+    def give(n):
+        piece = dsums[n % T, 1 - n // T]
+        square = jnp.sum(sums[n] * sums[n], axis=0).reshape(T, 8, CL).sum(axis=0)
+        squares[...] += sum(s[:, i : i + LANES] for s in (square, piece * piece) for i in range(0, s.shape[1], LANES))
+        for m in BOTH:
+            for j in range(SIZE):
+                going[j, n, pl.ds(PER * m, PER), :] = sums[n, m, pl.ds(PER * j, PER), :]
+        for j, device in co.group:
+            remote(going.at[j, n], rows_out.at[co.mine, n], xsems.at[0], xsems.at[1], device).start()
+        rows_out[co.mine, n] = going[co.mine, n]
+        if n >= T:
+            start_piece(dsums, down_out, co.index, dsems, way[n - T])
+
+    squares[...] = jnp.zeros_like(squares)
     for n in range(early):
         dsums[n, 1] = dsums1[n]
         for m in BOTH:
             sums[n, m] = sums1[n, m]
+        give(n)
     for copy in ins:
         copy.wait()
-    plan, scatters = Plan([]), []
+    plan, scatters, ends = Plan([]), [], []
 
     def start_scatter(swapped, start):
         def out(n, m):
             n += early
             return sums.at[n, m] if m < 2 else dsums.at[n % T, 1 - n // T]
 
-        scatter_stage(plan, scatters, co, (wide_s, down_s), scratch, out, swapped, T + 1, T + 1, T, start)
+        scatter_stage(plan, scatters, co, (wide_s, down_s), scratch, out, swapped, LATE, LATE, T, start)
+        ends.append(Stream([(s, "end") for s in scatters[-1]]))
+        ends[-1].add(functools.partial(give, early + len(ends) - 1))
+        ends[-1].mark("end")
+        plan.streams.append(ends[-1])
 
     start_scatter(False, 0.0)
     for b in range(blocks):
         if b and b % NB == 0:
             start_scatter(True, plan.now + SETTLE)
-        for i in range(NC + 1):
+        for i in range(SLOTS):
             plan.slot(THIRD_US if i < NC else GRADIENTS_US)
             if i == NC and b and b % NB == 0:
                 plan.need([(s, "begun") for s in scatters[-1]])
@@ -845,7 +883,7 @@
     slots3 = plan.take()
     start_scatter(True, plan.now + SETTLE)
     plan.slot()
-    plan.need([(s, "end") for stage in scatters for s in stage])
+    plan.need([(s, "end") for s in ends])
 
     def block3(b):
         for copy in down(b):
@@ -857,7 +895,7 @@
                 copy.start()
 
         def chunk(i):
-            run_slot(slots3, b * (NC + 1) + i)
+            run_slot(only(slots3, SLOTS, range(NC)), b * SLOTS + i)
             for copy in saved(b, i):
                 copy.wait()
             r = rows_of(i)
@@ -875,34 +913,14 @@
                     copy.start()
 
         loop(NC, chunk)
-        run_slot(slots3, b * (NC + 1) + NC)
-        gradients_step(co, (at_s, dh_ref, dgate_s, dup_s, hid_t), (wide_s, down_s), scratch, 1 + lax.div(b, NB), lax.rem(b, NB), T)
+        run_slot(only(slots3, SLOTS, [NC]), b * SLOTS + NC)
+        gradients_step(co, (at_s, dh_ref, dgate_s, dup_s, hid_t), (wide_s, down_s), scratch, 1 + lax.div(b, NB), lax.rem(b, NB), T, lambda: run_slot(only(slots3, SLOTS, [NC + 1]), b * SLOTS + NC + 1))
 
     loop(blocks, block3)
     for tick in plan.take()[0]:
         tick()
-    finish(co, sums, dsums, going, rows_out, down_out, total_out, (slots_a, slots_b), planes, xsems, psems, dsems)
-
-
-def finish(co, sums, dsums, going, rows_out, down_out, total_out, planes, groups, xsems, psems, dsems):
-    mine, here = co.mine, co.index
-    stages = sums.shape[0]
-    start_pieces(dsums, down_out, here, dsems, False)
-
-    def fill(n):
-        for m in BOTH:
-            for j in range(SIZE):
-                going[j, n, pl.ds(PER * m, PER), :] = sums[n, m, pl.ds(PER * j, PER), :]
-
-    loop(stages, fill)
-    copies = [remote(going.at[j], rows_out.at[mine], xsems.at[0], xsems.at[1], device) for j, device in co.group]
-    for copy in copies:
-        copy.start()
-    rows_out[pl.ds(mine, 1)] = going[pl.ds(mine, 1)]
-    square = jnp.sum((sums[...] * sums[...]).reshape(-1, 8, CL), axis=0)
-    piece = jnp.sum((dsums[...] * dsums[...]).reshape(-1, 8, D), axis=0)
-    square = sum(s[:, i : i + LANES] for s in (square, piece) for i in range(0, s.shape[1], LANES))
-    for n, (slots, (me, peers)) in enumerate(zip(planes, groups)):
+    square = squares[...]
+    for n, (slots, (me, peers)) in enumerate(zip((slots_a, slots_b), planes)):
         slots[me] = square
         for device in peers:
             remote(slots.at[me], slots.at[me], psems.at[2 * n], psems.at[2 * n + 1], device).start()
@@ -914,7 +932,7 @@
     rest = rows_out.at[upto(SIZE - 1)]
     for n in BOTH:
         await_bytes(rest, xsems.at[n])
-    await_pieces(dsums, down_out, here, dsems, False)
+    await_pieces(dsums, down_out, co.index, dsems, False)
 
 
 def hbm():
@@ -939,7 +957,7 @@
         out_shape=full * 2 + [kept] * 2 + [jax.ShapeDtypeStruct(s, bf16) for s in (FLAT, TALL)] + partial + [jax.ShapeDtypeStruct(XYZ + s, bf16) for s in SHAPES] + small,
         in_specs=[vmem(), vmem(), hbm(), hbm()],
         out_specs=[hbm()] * 15 + [vmem()] * 2,
-        scratch_shapes=scatter_scratch(DEEP)
+        scratch_shapes=scatter_scratch(DEEP, T)
         + [
             pltpu.VMEM(rows.shape, f32),
             pltpu.VMEM(CHUNK, f32),
@@ -956,8 +974,8 @@
             pltpu.VMEM((2,) + WIDE, bf16),
             pltpu.VMEM((2,) + DIMS[1:] + PIECE, bf16),
             pltpu.VMEM((NC, 2, RC, FB), f32),
-            pltpu.VMEM((DEEP + 1, 2) + XYZ + CHUNK, bf16),
-            pltpu.VMEM((DEEP + 1,) + XYZ + PIECE, bf16),
+            pltpu.VMEM((T, 2) + XYZ + CHUNK, bf16),
+            pltpu.VMEM((T,) + XYZ + PIECE, bf16),
         ]
         + [pltpu.SemaphoreType.DMA(s) for s in ((stages, 3, SEMS), (2, 3, 2), (NC, 2), (2,), (4,), (stages,))],
         compiler_params=pltpu.CompilerParams(collective_id=1, has_side_effects=True, vmem_limit_bytes=VMEM),
@@ -972,7 +990,7 @@
         out_shape=[jax.ShapeDtypeStruct(s, f32) for s in (shape, (T, 2) + PIECE, (8, LANES))],
         in_specs=[hbm()] * 9 + [vmem()] * 3,
         out_specs=[vmem()] * 3,
-        scratch_shapes=scatter_scratch(T)
+        scratch_shapes=scatter_scratch(T, LATE)
         + [
             pltpu.VMEM(FLAT, bf16),
             pltpu.VMEM(BLOCK, bf16),
@@ -980,10 +998,10 @@
             pltpu.VMEM(BLOCK[::-1], bf16),
             pltpu.VMEM((2,) + DIMS[1:] + PIECE, bf16),
             pltpu.VMEM((NC, 2, RC, FB), f32),
-            pltpu.VMEM((T + 1, 2) + XYZ + CHUNK, bf16),
-            pltpu.VMEM((T + 1,) + XYZ + PIECE, bf16),
+            pltpu.VMEM((LATE, 2) + XYZ + CHUNK, bf16),
+            pltpu.VMEM((LATE,) + XYZ + PIECE, bf16),
         ]
-        + [pltpu.VMEM(s, f32) for s in ((2 * T, 2) + CHUNK, (T, 2) + PIECE, shape, planes, planes)]
+        + [pltpu.VMEM(s, f32) for s in ((2 * T, 2) + CHUNK, (T, 2) + PIECE, shape, planes, planes, planes[1:])]
         + [pltpu.SemaphoreType.DMA(s) for s in ((2, 3, 2), (NC, 2), (2 * T,), (4,), (4,), (2 * T,))],
         compiler_params=pltpu.CompilerParams(collective_id=2, has_side_effects=True, vmem_limit_bytes=VMEM),
         name="backward",

time: 434 us -> 394 us (0.908)
  Pallas kernels: 421 us -> 382 us
    pallas_call x1, Pallas kernels: 279 us -> 245 us  [forward(): pl.pallas_call(forward_kernel, out_shape=full * 2 + [kept] * 2 + [jax.Sha...]
    pallas_call x1, Pallas kernels: 142 us -> 137 us  [backward(): pl.pallas_call(backward_kernel, out_shape=[jax.ShapeDtypeStruct(s, f32) f...]
where the time goes in v3:
time: 394 us
  Pallas kernels  382 us (97%)
  other arithmetic  5.81 us (1%)
  local copies, waits for them, and re-layouts  4.47 us (1%)
    pallas_call x1, Pallas kernels, forward(): pl.pallas_call(forward_kernel, out_shape=full * 2 + [kept] * 2 + [jax.Sha...  245 us
    pallas_call x1, Pallas kernels, backward(): pl.pallas_call(backward_kernel, out_shape=[jax.ShapeDtypeStruct(s, f32) f...  137 us

profile of v3, /device:TPU:1, one launch (start us, length us, event | category | flops | bytes accessed | tf_op | source)
XLA Modules:
  0.0 393.7 jit_solution(17272469019889444410)
XLA Ops:
  0.6 1.5 copy_bitcast_fusion.down_ref
  2.2 1.1 pad_maximum_fusion
  3.3 0.1 convert_element_type.31
  3.5 0.8 pad_convert_fusion.rows_ref
  4.3 244.9 %forward.1 = (bf16[3,4,4,8,2,24,256]{6,5,4,3,2,1,0:T(8,128)(2,1)}, bf16[3,4,4,8,2,24,256]{6,5,4,3,2,1,0:T(8,128)(2,1)}, bf16[3,4,4,8,2,8,768]{6,5,4,3,2,1,0:T(8,...) custom-call(f32[8,6,8,256]{3,2,1,0:T(8,128)} %pad_convert_fusion.row, ...), custom_call_target="tpu_custom_call" | custom-call | tf_op jit(solution)/shard_map/forward/pallas_call | solution.py:955
  249.2 137.0 %backward.1 = (f32[8,6,8,256]{3,2,1,0:T(8,128)}, f32[3,2,8,768]{3,2,1,0:T(8,128)}, f32[8,128]{1,0:T(8,128)}) custom-call(bf16[3,4,4,8,2,8,768]{6,5,4,3,2,1,0:T(8,128)(2,1)} %get-tuple-element.24.down1, f32[12,2,512,512]{3,2,1,0:T(8,128)} %get-tuple-element.25.gate_ref, f32[12,2,512,512]{3,2,1,0:T(8,128)} %get-tuple-element.26.up_ref, ...), custom_call_target="tpu_custom_call" | custom-call | tf_op jit(solution)/shard_map/backward/pallas_call | solution.py:988
  386.2 0.0 copy-start.6
  386.2 0.0 copy-start.7
  386.3 0.0 copy-start
  386.3 0.0 copy-start.2
  386.3 0.0 copy-start.3
  386.3 0.0 copy-start.1
  386.3 0.0 copy-start.4
  386.3 0.0 copy-start.5
  386.3 1.3 slice.23
  388.4 1.2 copy.29
  389.6 0.1 mul.125
  389.7 0.1 mul.115
  389.8 0.0 copy-done.6
  389.9 0.0 copy-done.7
  389.9 0.0 copy-done.8
  389.9 1.6 fusion.6
  391.5 1.1 fusion.11
  392.6 1.1 fusion.12
  (12 shorter events, 0.1 us)
Async XLA Ops:
  386.2 3.6 copy-start.6
  386.2 3.6 copy-start.7
  386.2 3.6 copy-start.8
  386.3 5.3 %copy-start = (bf16[2,3,6144]{2,0,1:T(2,128)(2,1)S(1)}, bf16[2,3,6144]{2,0,1:T(2,128)(2,1)}, u32[]{:S(2)}) copy-start(bf16[2,3,6144]{2,0,1:T(2,128)(2,1)} %param.13) | copy-start | bytes 221188
  386.3 5.3 %copy-start.2 = (f32[2,3,6144]{2,0,1:T(2,128)S(1)}, f32[2,3,6144]{2,0,1:T(2,128)}, u32[]{:S(2)}) copy-start(f32[2,3,6144]{2,0,1:T(2,128)} %param.19) | copy-start | bytes 442372
  386.3 5.2 %copy-start.3 = (f32[2,3,6144]{2,0,1:T(2,128)S(1)}, f32[2,3,6144]{2,0,1:T(2,128)}, u32[]{:S(2)}) copy-start(f32[2,3,6144]{2,0,1:T(2,128)} %param.16) | copy-start | bytes 442372
  386.3 6.3 %copy-start.1 = (bf16[2,3,6144]{2,0,1:T(2,128)(2,1)S(1)}, bf16[2,3,6144]{2,0,1:T(2,128)(2,1)}, u32[]{:S(2)}) copy-start(bf16[2,3,6144]{2,0,1:T(2,128)(2,1)} %param.14) | copy-start | bytes 221188
  386.3 6.3 %copy-start.4 = (f32[2,3,6144]{2,0,1:T(2,128)S(1)}, f32[2,3,6144]{2,0,1:T(2,128)}, u32[]{:S(2)}) copy-start(f32[2,3,6144]{2,0,1:T(2,128)} %param.20) | copy-start | bytes 442372
  386.3 6.3 %copy-start.5 = (f32[2,3,6144]{2,0,1:T(2,128)S(1)}, f32[2,3,6144]{2,0,1:T(2,128)}, u32[]{:S(2)}) copy-start(f32[2,3,6144]{2,0,1:T(2,128)} %param.17) | copy-start | bytes 442372
